TPU v7x, 32 devices: a whole 2x2x4 slice. The times are simulated.
32 devices in a mesh: cp: 32 (over z, y, x, core).
Axes of the slice: x: 2, y: 2, z: 4, core: 2. Of those that a mesh axis runs over, the one named last changes fastest.
Arguments:
- x_seq: bfloat16 [1, 24576, 64, 64], P(None, 'cp')
- dt_seq: float32 [1, 24576, 64], P(None, 'cp')
- a_log: float32 [64], replicated
- b_proj: bfloat16 [1, 24576, 128], P(None, 'cp')
- c_proj: bfloat16 [1, 24576, 128], P(None, 'cp')
- d_skip: float32 [64], replicated
- s_init: float32 [1, 64, 64, 128], replicated
- dy_seq: bfloat16 [1, 24576, 64, 64], P(None, 'cp')
- ds_last: float32 [1, 64, 64, 128], replicated
Outputs:
- output 1: bfloat16 [1, 24576, 64, 64], P(None, 'cp')
- output 2: float32 [1, 24576, 64], P(None, 'cp')
- output 3: bfloat16 [1, 24576, 128], P(None, 'cp')
- output 4: bfloat16 [1, 24576, 128], P(None, 'cp')
- output 5: float32 [1, 64, 64, 128], replicated
- output 6: float32 [64], replicated
- output 7: float32 [64], replicated
All inputs are finite; a program needn't handle non-finite values.
Results may differ from a plain program's by a relative error of at most 0.001.
Values sent between devices are 32-bit elements.
A program may use at most 1 GiB of HBM per device.

v0:
```python
import functools
import jax
import jax.numpy as jnp
from jax import lax
from jax.sharding import PartitionSpec as P, NamedSharding

CHUNK = 256
AXIS = 'cp'
HIGH_PREC = lax.Precision.HIGHEST


def chunk_step(carry_state, blk_in, neg_rate, d_skip):
    x_blk, dt_blk, b_blk, c_blk = blk_in
    cum_decay = jnp.cumsum(dt_blk * neg_rate, axis=1)
    u_blk = x_blk * dt_blk[..., None]
    gram_mat = jnp.einsum('btn,bsn->bts', c_blk, b_blk, precision=HIGH_PREC, preferred_element_type=jnp.float32)
    blk_len = x_blk.shape[1]
    causal = (jnp.arange(blk_len)[:, None] >= jnp.arange(blk_len)[None, :])[None, :, :, None]
    log_diff = jnp.where(causal, cum_decay[:, :, None, :] - cum_decay[:, None, :, :], 0.0)
    mix_mat = jnp.where(causal, jnp.exp(log_diff), 0.0) * gram_mat[..., None]
    y_blk = jnp.einsum('btsh,bshp->bthp', mix_mat, u_blk, precision=HIGH_PREC, preferred_element_type=jnp.float32)
    y_blk = y_blk + jnp.exp(cum_decay)[..., None] * jnp.einsum('bhpn,btn->bthp', carry_state, c_blk, precision=HIGH_PREC, preferred_element_type=jnp.float32)
    y_blk = y_blk + d_skip[:, None] * x_blk
    tail_decay = jnp.exp(cum_decay[:, -1:, :] - cum_decay)
    new_state = jnp.exp(cum_decay[:, -1, :])[..., None, None] * carry_state + jnp.einsum('bsh,bshp,bsn->bhpn', tail_decay, u_blk, b_blk, precision=HIGH_PREC, preferred_element_type=jnp.float32)
    return new_state, y_blk


def ssd_forward(x_seq, dt_seq, a_log, b_proj, c_proj, d_skip, s_init, n_span):
    n_batch, seq_len = x_seq.shape[0], x_seq.shape[1]
    per_span = seq_len // (n_span * CHUNK)
    neg_rate = -jnp.exp(a_log)
    inner_step = jax.checkpoint(functools.partial(chunk_step, neg_rate=neg_rate, d_skip=d_skip))

    def span_step(carry_state, span_in):
        return lax.scan(inner_step, carry_state, span_in)

    def split_seq(array_in):
        blocks = array_in.astype(jnp.float32).reshape((n_batch, n_span, per_span, CHUNK) + array_in.shape[2:])
        return jnp.moveaxis(blocks, 0, 2)

    seq_in = (split_seq(x_seq), split_seq(dt_seq), split_seq(b_proj), split_seq(c_proj))
    final_state, y_blocks = lax.scan(jax.checkpoint(span_step), s_init, seq_in)
    y_seq = jnp.moveaxis(y_blocks, 2, 0).reshape(x_seq.shape)
    return y_seq, final_state


def shard_summary(x_loc, dt_loc, a_log, b_loc, c_loc, dy_loc):
    cum_decay = jnp.cumsum(dt_loc * (-jnp.exp(a_log)), axis=1)
    log_total = cum_decay[:, -1, :]
    in_weight = jnp.exp(log_total[:, None, :] - cum_decay) * dt_loc
    x_weighted = x_loc.astype(jnp.float32) * in_weight[..., None]
    state_part = jnp.einsum('bthp,btn->bhpn', x_weighted, b_loc.astype(jnp.float32), precision=HIGH_PREC, preferred_element_type=jnp.float32)
    dy_weighted = dy_loc.astype(jnp.float32) * jnp.exp(cum_decay)[..., None]
    grad_part = jnp.einsum('bthp,btn->bhpn', dy_weighted, c_loc.astype(jnp.float32), precision=HIGH_PREC, preferred_element_type=jnp.float32)
    return state_part, grad_part, log_total


def link_states(state_all, grad_all, logdec_all, dev_idx, s_init, ds_last):
    log_before = jnp.cumsum(logdec_all, axis=0) - logdec_all
    log_total = jnp.sum(logdec_all, axis=0)
    log_here = log_before[dev_idx]
    log_after = log_here + logdec_all[dev_idx]
    dev_order = jnp.arange(logdec_all.shape[0])[:, None, None]
    w_left = jnp.where(dev_order < dev_idx, jnp.exp(jnp.minimum(log_here[None] - log_before - logdec_all, 0.0)), 0.0)
    s_start = jnp.exp(log_here)[..., None, None] * s_init + jnp.einsum('jbh,jbhpn->bhpn', w_left, state_all, precision=HIGH_PREC, preferred_element_type=jnp.float32)
    w_right = jnp.where(dev_order > dev_idx, jnp.exp(jnp.minimum(log_before - log_after[None], 0.0)), 0.0)
    ds_end = jnp.exp(log_total - log_after)[..., None, None] * ds_last + jnp.einsum('jbh,jbhpn->bhpn', w_right, grad_all, precision=HIGH_PREC, preferred_element_type=jnp.float32)
    ds_first = jnp.exp(log_total)[..., None, None] * ds_last + jnp.einsum('jbh,jbhpn->bhpn', jnp.exp(log_before), grad_all, precision=HIGH_PREC, preferred_element_type=jnp.float32)
    return s_start, ds_end, ds_first


def solution(mesh):
    tok4 = P(None, AXIS, None, None)
    tok3 = P(None, AXIS, None)

    def device_step(x_loc, dt_loc, a_log, b_loc, c_loc, d_skip, s_init, dy_loc, ds_last):
        dev_idx = lax.axis_index(AXIS)
        state_part, grad_part, log_part = shard_summary(x_loc, dt_loc, a_log, b_loc, c_loc, dy_loc)
        state_all = lax.all_gather(state_part, AXIS)
        grad_all = lax.all_gather(grad_part, AXIS)
        logdec_all = lax.all_gather(log_part, AXIS)
        s_start, ds_end, ds_first = link_states(state_all, grad_all, logdec_all, dev_idx, s_init, ds_last)

        def local_forward(x_in, dt_in, alog_in, b_in, c_in, skip_in):
            return ssd_forward(x_in, dt_in, alog_in, b_in, c_in, skip_in, s_start, 1)

        _, pull_back = jax.vjp(local_forward, x_loc, dt_loc, a_log, b_loc, c_loc, d_skip)
        grad_x, grad_dt, grad_alog, grad_b, grad_c, grad_skip = pull_back((dy_loc.astype(jnp.float32), ds_end))
        grad_alog, grad_skip = lax.psum((grad_alog, grad_skip), AXIS)
        return grad_x, grad_dt, grad_b, grad_c, ds_first, grad_alog, grad_skip

    return jax.shard_map(device_step, mesh=mesh,
                         in_specs=(tok4, tok3, P(), tok3, tok3, P(), P(), tok4, P()),
                         out_specs=(tok4, tok3, tok3, tok3, P(), P(), P()),
                         check_vma=False)
```

profile of v0, /device:TPU:0, one launch (start us, length us, event | category | flops | bytes accessed | tf_op | source)
XLA Modules:
  0.0 1285.9 jit_solution(18366543977035341739)
XLA Ops:
  11.3 9.5 fusion.102
  21.2 9.5 fusion.104
  30.7 18.5 %squeeze.118 = f32[3,1,256,64,64]{2,0,4,3,1:T(4,128)} reshape(bf16[1,768,64,64]{1,3,2,0:T(8,128)(2,1)} %param.13) | data formatting | bytes 18874368 | tf_op jit(solution)/shard_map/transpose(jvp())/while/body/jit(dynamic_index_in_dim)/squeeze | solution.py:43
  49.2 18.5 %squeeze.125 = f32[3,1,256,64,64]{2,0,4,3,1:T(4,128)} reshape(bf16[1,768,64,64]{1,3,2,0:T(8,128)(2,1)} %param.20) | data formatting | bytes 18874368 | tf_op jit(solution)/shard_map/transpose(jvp())/while/body/jit(dynamic_index_in_dim)/squeeze | solution.py:43
  68.6 43.8 %all_gather.15 = f32[32,1,64]{2,1,0:T(1,128)S(1)} all-gather(f32[1,1,64]{2,1,0:T(1,128)S(1)} %copy.159), channel_id=1, replica_groups=mesh['cp'=32] {'cp'}, dimensions={0}, use_global_device_ids=true | all-gather | bytes 8448 | tf_op jit(solution)/shard_map/all_gather | solution.py:82
  113.7 265.2 %all-gather.7.cloned.1.call-done = f32[2048,64,128]{2,1,0:T(8,128)} async-done(((f32[64,64,128]{2,1,0:T(8,128)}), f32[2048,64,128]{2,1,0:T(8,128)}) %all-gather.7.cloned.1.call-update) | async-done | bytes 67108880 | tf_op jit(solution)/shard_map/all_gather | solution.py:81
  378.9 84.6 %fusion.100 = f32[64,1,64,128]{3,1,2,0:T(1,128)} fusion(f32[32,64,1,1]{0,2,3,1:T(1,128)S(1)} %copy.175, f32[32,64,64,128]{3,2,1,0:T(8,128)} %bitcast.37), kind=kOutput, calls=%fused_computation.133 | convolution fusion | flops 201326592 | bytes 69214208 | tf_op jit(solution)/shard_map/jbh,jbhpn->bhpn/dot_general | solution.py:68
  463.5 85.0 %fusion.98 = f32[64,1,64,128]{3,1,2,0:T(1,128)} fusion(f32[32,64,1,1]{0,2,3,1:T(1,128)S(1)} %copy.178, f32[32,64,64,128]{3,2,1,0:T(8,128)} %bitcast.37), kind=kOutput, calls=%fused_computation.131 | convolution fusion | flops 201326592 | bytes 69214208 | tf_op jit(solution)/shard_map/jbh,jbhpn->bhpn/dot_general | solution.py:69
  548.6 187.1 %all-gather.5.cloned.1.call-done = f32[2048,64,128]{2,1,0:T(8,128)} async-done(((f32[64,64,128]{2,1,0:T(8,128)}), f32[2048,64,128]{2,1,0:T(8,128)}) %all-gather.5.cloned.1.call-update) | async-done | bytes 67108880 | tf_op jit(solution)/shard_map/all_gather | solution.py:80
  735.7 83.2 %fusion.96 = f32[64,1,64,128]{3,1,2,0:T(1,128)S(1)} fusion(f32[32,64,1,1]{0,2,3,1:T(1,128)S(1)} %copy.172, f32[32,64,64,128]{3,2,1,0:T(8,128)} %bitcast.23), kind=kOutput, calls=%fused_computation.129 | convolution fusion | flops 201326592 | bytes 69214208 | tf_op jit(solution)/shard_map/jbh,jbhpn->bhpn/dot_general | solution.py:66
  824.2 12.8 copy.160
  837.0 42.7 %while.73 = (s32[]{:T(128)}, f32[1,64,64,128]{3,2,1,0:T(8,128)}, f32[3,1,64,64,128]{4,3,2,1,0:T(8,128)}, f32[3,1,256,64]{2,0,3,1:T(4,128)}, f32[1,1,64]{2,1,0:T(...) while((s32[]{:T(128)}, f32[1,64,64,128]{3,2,1,0:T(8,128)}, ...), condition=%wide.region_7.8_spmd, body=%wide.region_4.7_spmd.sunk | while | flops 1615888640 | bytes 14098793 | solution.py:36
  843.6 7.6 bitcast_add_fusion.12
  857.9 7.6 bitcast_add_fusion.12
  872.1 7.6 bitcast_add_fusion.12
  885.3 346.4 %while.74 = (s32[]{:T(128)}, f32[64]{0:T(128)}, f32[64]{0:T(128)}, f32[1,64,64,128]{3,2,1,0:T(8,128)S(1)}, bf16[3,1,256,64,64]{2,4,3,1,0:T(8,128)(2,1)}, /*index...) while((s32[]{:T(128)}, f32[64]{0:T(128)}, f32[64]{0:T(128)}, ...), condition=%wide.region_22.23_spmd.clone, body=%wide.region_8.22_spmd.clone.sunk | while | flops 14886912000 | bytes 181818704 | solution.py:36
  908.9 7.4 constant_dynamic-slice_fusion.6
  916.3 6.6 copy_bitcast_fusion.6
  929.3 9.3 fusion.182
  939.2 28.5 %fusion.175 = (f32[256,64]{0,1:T(8,128)}, f32[256,64]{0,1:T(8,128)}, f32[256,256]{1,0:T(8,128)S(1)}) fusion(f32[256,64]{0,1:T(8,128)S(1)} %copy.237, f32[256,256]{1,0:T(8,128)S(1)} %fusion.172, pred[256,256]{1,0:T(8,128)(4,1)S(1)} %iota_compare_fusion.4, f32[1,256,64,64]{1,3,2,0:T(8,128)} %get-tuple-element.928, f32[256,64]{0,1:T(8,128)S(1)} %bitcast.511, ...), kind=kOutput, calls=%fused_computation.34.clone.1 | convolution fusion | flops 3268313088 | bytes 9240576 | tf_op jit(solution)/shard_map/transpose(jvp())/while/body/eval_jaxpr/checkpoint/while/body/eval_jaxpr/checkpoint/btsh,bshp->bthp/dot_general | solution.py:21
  975.7 18.7 %multiply_reduce_fusion.6 = (f32[256,64]{0,1:T(8,128)}, f32[64]{0:T(128)}, f32[1,256,64,64]{1,3,2,0:T(8,128)S(1)}) fusion(f32[1,256,64,64]{1,3,2,0:T(8,128)} %get-tuple-element.928, f32[1,256,64,64]{1,3,2,0:T(8,128)} %get-tuple-element.929, f32[256,256]{1,0:T(8,128)} %copy-done.6, f32[256,64]{0,1:T(8,128)} %copy-done.13, ...), kind=kOutput, calls=%fused_computation.58.clone.1 | convolution fusion | flops 3244277760 | bytes 17301760 | tf_op jit(solution)/shard_map/transpose(jvp())/while/body/eval_jaxpr/checkpoint/while/body/eval_jaxpr/checkpoint/btsh,bshp->bthp/dot_general | solution.py:21
  1016.5 7.4 constant_dynamic-slice_fusion.6
  1023.9 6.6 copy_bitcast_fusion.6
  1036.9 9.3 fusion.182
  1046.8 28.5 %fusion.175 = (f32[256,64]{0,1:T(8,128)}, f32[256,64]{0,1:T(8,128)}, f32[256,256]{1,0:T(8,128)S(1)}) fusion(f32[256,64]{0,1:T(8,128)S(1)} %copy.237, f32[256,256]{1,0:T(8,128)S(1)} %fusion.172, pred[256,256]{1,0:T(8,128)(4,1)S(1)} %iota_compare_fusion.4, f32[1,256,64,64]{1,3,2,0:T(8,128)} %get-tuple-element.928, f32[256,64]{0,1:T(8,128)S(1)} %bitcast.511, ...), kind=kOutput, calls=%fused_computation.34.clone.1 | convolution fusion | flops 3268313088 | bytes 9240576 | tf_op jit(solution)/shard_map/transpose(jvp())/while/body/eval_jaxpr/checkpoint/while/body/eval_jaxpr/checkpoint/btsh,bshp->bthp/dot_general | solution.py:21
  1083.3 18.7 %multiply_reduce_fusion.6 = (f32[256,64]{0,1:T(8,128)}, f32[64]{0:T(128)}, f32[1,256,64,64]{1,3,2,0:T(8,128)S(1)}) fusion(f32[1,256,64,64]{1,3,2,0:T(8,128)} %get-tuple-element.928, f32[1,256,64,64]{1,3,2,0:T(8,128)} %get-tuple-element.929, f32[256,256]{1,0:T(8,128)} %copy-done.6, f32[256,64]{0,1:T(8,128)} %copy-done.13, ...), kind=kOutput, calls=%fused_computation.58.clone.1 | convolution fusion | flops 3244277760 | bytes 17301760 | tf_op jit(solution)/shard_map/transpose(jvp())/while/body/eval_jaxpr/checkpoint/while/body/eval_jaxpr/checkpoint/btsh,bshp->bthp/dot_general | solution.py:21
  1124.1 7.4 constant_dynamic-slice_fusion.6
  1131.5 6.6 copy_bitcast_fusion.6
  1144.5 9.3 fusion.182
  1154.4 28.5 %fusion.175 = (f32[256,64]{0,1:T(8,128)}, f32[256,64]{0,1:T(8,128)}, f32[256,256]{1,0:T(8,128)S(1)}) fusion(f32[256,64]{0,1:T(8,128)S(1)} %copy.237, f32[256,256]{1,0:T(8,128)S(1)} %fusion.172, pred[256,256]{1,0:T(8,128)(4,1)S(1)} %iota_compare_fusion.4, f32[1,256,64,64]{1,3,2,0:T(8,128)} %get-tuple-element.928, f32[256,64]{0,1:T(8,128)S(1)} %bitcast.511, ...), kind=kOutput, calls=%fused_computation.34.clone.1 | convolution fusion | flops 3268313088 | bytes 9240576 | tf_op jit(solution)/shard_map/transpose(jvp())/while/body/eval_jaxpr/checkpoint/while/body/eval_jaxpr/checkpoint/btsh,bshp->bthp/dot_general | solution.py:21
  1190.9 18.7 %multiply_reduce_fusion.6 = (f32[256,64]{0,1:T(8,128)}, f32[64]{0:T(128)}, f32[1,256,64,64]{1,3,2,0:T(8,128)S(1)}) fusion(f32[1,256,64,64]{1,3,2,0:T(8,128)} %get-tuple-element.928, f32[1,256,64,64]{1,3,2,0:T(8,128)} %get-tuple-element.929, f32[256,256]{1,0:T(8,128)} %copy-done.6, f32[256,64]{0,1:T(8,128)} %copy-done.13, ...), kind=kOutput, calls=%fused_computation.58.clone.1 | convolution fusion | flops 3244277760 | bytes 17301760 | tf_op jit(solution)/shard_map/transpose(jvp())/while/body/eval_jaxpr/checkpoint/while/body/eval_jaxpr/checkpoint/btsh,bshp->bthp/dot_general | solution.py:21
  1240.2 38.5 %all-reduce.2 = (f32[64]{0:T(128)}, f32[64]{0:T(128)}) all-reduce(f32[64]{0:T(128)S(1)} %negate_multiply_fusion, f32[64]{0:T(128)S(1)} %copy-done.28), channel_id=1, replica_groups=mesh['cp'=32] {'cp'}, use_global_device_ids=true, to_apply=%region_23.24 | all-reduce | flops 128 | bytes 1024 | tf_op jit(solution)/shard_map/psum | solution.py:90
  (370 shorter events, 155.8 us)
Async XLA Ops:
  7.2 371.7 %all-gather.7.cloned.1.call-start = ((), (), s32[]{:S(2)}) async-start(), calls=%async_computation.1 | async-start | bytes 69206016 | tf_op jit(solution)/shard_map/all_gather | solution.py:81
  20.8 714.8 %all-gather.5.cloned.1.call-start = ((), (), s32[]{:S(2)}) async-start(), calls=%async_computation | async-start | bytes 69206016 | tf_op jit(solution)/shard_map/all_gather | solution.py:80
  49.2 63.7 %copy-start.20 = (bf16[1,768,128]{2,1,0:T(8,128)(2,1)S(1)}, bf16[1,768,128]{2,1,0:T(8,128)(2,1)}, u32[]{:S(2)}) copy-start(bf16[1,768,128]{2,1,0:T(8,128)(2,1)} %param.17) | copy-start | bytes 589828
  735.7 83.2 %copy-start.7 = (f32[1,64,64,128]{3,2,1,0:T(8,128)S(1)}, f32[1,64,64,128]{3,2,1,0:T(8,128)}, u32[]{:S(2)}) copy-start(f32[1,64,64,128]{3,2,1,0:T(8,128)} %param.19) | copy-start | bytes 6291460
  938.7 29.0 %copy-start.13 = (f32[256,64]{0,1:T(8,128)}, f32[256,64]{0,1:T(8,128)S(1)}, u32[]{:S(2)}) copy-start(f32[256,64]{0,1:T(8,128)S(1)} %copy.237) | copy-start | bytes 196612 | tf_op jit(solution)/shard_map/transpose(jvp())/while/body/eval_jaxpr/checkpoint/while
  939.1 28.6 %copy-start.6 = (f32[256,256]{1,0:T(8,128)}, f32[256,256]{1,0:T(8,128)S(1)}, u32[]{:S(2)}) copy-start(f32[256,256]{1,0:T(8,128)S(1)} %fusion.172) | copy-start | bytes 786436 | tf_op jit(solution)/shard_map/transpose(jvp())/while/body/eval_jaxpr/checkpoint/while
  939.2 28.5 %copy-start.14 = (pred[256,256]{1,0:T(8,128)(4,1)}, pred[256,256]{1,0:T(8,128)(4,1)S(1)}, u32[]{:S(2)}) copy-start(pred[256,256]{1,0:T(8,128)(4,1)S(1)} %iota_compare_fusion.4) | copy-start | bytes 196612 | tf_op jit(solution)/shard_map/transpose(jvp())/while/body/eval_jaxpr/checkpoint/while
  939.2 28.5 %copy-start.21 = (bf16[3,1,256,128]{3,2,1,0:T(8,128)(2,1)S(1)}, bf16[3,1,256,128]{3,2,1,0:T(8,128)(2,1)}, u32[]{:S(2)}) copy-start(bf16[3,1,256,128]{3,2,1,0:T(8,128)(2,1)} %get-tuple-element.1007) | copy-start | bytes 589828 | tf_op jit(solution)/shard_map/transpose(jvp())/while/body/eval_jaxpr/checkpoint/while
  939.2 28.9 %copy-start.1 = (f32[1,256,64,64]{1,3,2,0:T(8,128)S(1)}, f32[1,256,64,64]{1,3,2,0:T(8,128)}, u32[]{:S(2)}) copy-start(f32[1,256,64,64]{1,3,2,0:T(8,128)} %get-tuple-element.928) | copy-start | bytes 12582916 | tf_op jit(solution)/shard_map/transpose(jvp())/while/body/eval_jaxpr/checkpoint/while
  975.7 18.7 %copy-start = (f32[1,256,64,64]{1,3,2,0:T(8,128)S(1)}, f32[1,256,64,64]{1,3,2,0:T(8,128)}, u32[]{:S(2)}) copy-start(f32[1,256,64,64]{1,3,2,0:T(8,128)} %get-tuple-element.929) | copy-start | bytes 12582916 | tf_op jit(solution)/shard_map/transpose(jvp())/while/body/eval_jaxpr/checkpoint/while
  975.7 18.7 %copy-start.23 = (f32[64]{0:T(128)S(1)}, f32[64]{0:T(128)}, u32[]{:S(2)}) copy-start(f32[64]{0:T(128)} %get-tuple-element.950) | copy-start | bytes 772 | tf_op jit(solution)/shard_map/transpose(jvp())/while/body/eval_jaxpr/checkpoint/while
  1005.7 10.2 copy-start.26
  1005.7 10.2 copy-start.29
  1046.3 29.0 %copy-start.13 = (f32[256,64]{0,1:T(8,128)}, f32[256,64]{0,1:T(8,128)S(1)}, u32[]{:S(2)}) copy-start(f32[256,64]{0,1:T(8,128)S(1)} %copy.237) | copy-start | bytes 196612 | tf_op jit(solution)/shard_map/transpose(jvp())/while/body/eval_jaxpr/checkpoint/while
  1046.7 28.6 %copy-start.6 = (f32[256,256]{1,0:T(8,128)}, f32[256,256]{1,0:T(8,128)S(1)}, u32[]{:S(2)}) copy-start(f32[256,256]{1,0:T(8,128)S(1)} %fusion.172) | copy-start | bytes 786436 | tf_op jit(solution)/shard_map/transpose(jvp())/while/body/eval_jaxpr/checkpoint/while
  1046.7 28.5 %copy-start.14 = (pred[256,256]{1,0:T(8,128)(4,1)}, pred[256,256]{1,0:T(8,128)(4,1)S(1)}, u32[]{:S(2)}) copy-start(pred[256,256]{1,0:T(8,128)(4,1)S(1)} %iota_compare_fusion.4) | copy-start | bytes 196612 | tf_op jit(solution)/shard_map/transpose(jvp())/while/body/eval_jaxpr/checkpoint/while
  1046.8 28.5 %copy-start.21 = (bf16[3,1,256,128]{3,2,1,0:T(8,128)(2,1)S(1)}, bf16[3,1,256,128]{3,2,1,0:T(8,128)(2,1)}, u32[]{:S(2)}) copy-start(bf16[3,1,256,128]{3,2,1,0:T(8,128)(2,1)} %get-tuple-element.1007) | copy-start | bytes 589828 | tf_op jit(solution)/shard_map/transpose(jvp())/while/body/eval_jaxpr/checkpoint/while
  1046.8 28.9 %copy-start.1 = (f32[1,256,64,64]{1,3,2,0:T(8,128)S(1)}, f32[1,256,64,64]{1,3,2,0:T(8,128)}, u32[]{:S(2)}) copy-start(f32[1,256,64,64]{1,3,2,0:T(8,128)} %get-tuple-element.928) | copy-start | bytes 12582916 | tf_op jit(solution)/shard_map/transpose(jvp())/while/body/eval_jaxpr/checkpoint/while
  1083.3 18.7 %copy-start = (f32[1,256,64,64]{1,3,2,0:T(8,128)S(1)}, f32[1,256,64,64]{1,3,2,0:T(8,128)}, u32[]{:S(2)}) copy-start(f32[1,256,64,64]{1,3,2,0:T(8,128)} %get-tuple-element.929) | copy-start | bytes 12582916 | tf_op jit(solution)/shard_map/transpose(jvp())/while/body/eval_jaxpr/checkpoint/while
  1083.3 18.7 %copy-start.23 = (f32[64]{0:T(128)S(1)}, f32[64]{0:T(128)}, u32[]{:S(2)}) copy-start(f32[64]{0:T(128)} %get-tuple-element.950) | copy-start | bytes 772 | tf_op jit(solution)/shard_map/transpose(jvp())/while/body/eval_jaxpr/checkpoint/while
  1113.3 10.2 copy-start.26
  1113.3 10.2 copy-start.29
  1153.9 29.0 %copy-start.13 = (f32[256,64]{0,1:T(8,128)}, f32[256,64]{0,1:T(8,128)S(1)}, u32[]{:S(2)}) copy-start(f32[256,64]{0,1:T(8,128)S(1)} %copy.237) | copy-start | bytes 196612 | tf_op jit(solution)/shard_map/transpose(jvp())/while/body/eval_jaxpr/checkpoint/while
  1154.3 28.6 %copy-start.6 = (f32[256,256]{1,0:T(8,128)}, f32[256,256]{1,0:T(8,128)S(1)}, u32[]{:S(2)}) copy-start(f32[256,256]{1,0:T(8,128)S(1)} %fusion.172) | copy-start | bytes 786436 | tf_op jit(solution)/shard_map/transpose(jvp())/while/body/eval_jaxpr/checkpoint/while
  1154.3 28.5 %copy-start.14 = (pred[256,256]{1,0:T(8,128)(4,1)}, pred[256,256]{1,0:T(8,128)(4,1)S(1)}, u32[]{:S(2)}) copy-start(pred[256,256]{1,0:T(8,128)(4,1)S(1)} %iota_compare_fusion.4) | copy-start | bytes 196612 | tf_op jit(solution)/shard_map/transpose(jvp())/while/body/eval_jaxpr/checkpoint/while
  1154.3 28.5 %copy-start.21 = (bf16[3,1,256,128]{3,2,1,0:T(8,128)(2,1)S(1)}, bf16[3,1,256,128]{3,2,1,0:T(8,128)(2,1)}, u32[]{:S(2)}) copy-start(bf16[3,1,256,128]{3,2,1,0:T(8,128)(2,1)} %get-tuple-element.1007) | copy-start | bytes 589828 | tf_op jit(solution)/shard_map/transpose(jvp())/while/body/eval_jaxpr/checkpoint/while
  1154.3 28.9 %copy-start.1 = (f32[1,256,64,64]{1,3,2,0:T(8,128)S(1)}, f32[1,256,64,64]{1,3,2,0:T(8,128)}, u32[]{:S(2)}) copy-start(f32[1,256,64,64]{1,3,2,0:T(8,128)} %get-tuple-element.928) | copy-start | bytes 12582916 | tf_op jit(solution)/shard_map/transpose(jvp())/while/body/eval_jaxpr/checkpoint/while
  1190.9 18.7 %copy-start = (f32[1,256,64,64]{1,3,2,0:T(8,128)S(1)}, f32[1,256,64,64]{1,3,2,0:T(8,128)}, u32[]{:S(2)}) copy-start(f32[1,256,64,64]{1,3,2,0:T(8,128)} %get-tuple-element.929) | copy-start | bytes 12582916 | tf_op jit(solution)/shard_map/transpose(jvp())/while/body/eval_jaxpr/checkpoint/while
  1190.9 18.7 %copy-start.23 = (f32[64]{0:T(128)S(1)}, f32[64]{0:T(128)}, u32[]{:S(2)}) copy-start(f32[64]{0:T(128)} %get-tuple-element.950) | copy-start | bytes 772 | tf_op jit(solution)/shard_map/transpose(jvp())/while/body/eval_jaxpr/checkpoint/while
  1220.9 10.2 copy-start.24
  1220.9 10.2 copy-start.26
  1220.9 10.2 copy-start.29
  (40 other events, 179.0 us)
Sparse Core Ops, SparseCore 0:
  21.0 357.8 all-gather.6
  381.8 353.8 all-gather.4
where the time goes:
time: 1290 us
  matrix products  519 us (40%)
  waiting for transfers between devices  452 us (35%)
  local copies, waits for them, and re-layouts  153 us (12%)
  blocking collectives  82.2 us (6%)
  other arithmetic  39.3 us (3%)
  loops' own time  25.1 us (2%)
  between operations  14.6 us (1%)
    all_gather x1, waiting for transfers between devices, device_step(): grad_all = lax.all_gather(grad_part, AXIS)  265 us
    all_gather x1, waiting for transfers between devices, device_step(): state_all = lax.all_gather(state_part, AXIS)  187 us
    dot_general x6, matrix products, chunk_step(): jnp.einsum('btsh,bshp->bthp', mix_mat, u_blk, precision=HIGH_PREC, prefer...  141 us
    dot_general x1, matrix products, link_states(): jnp.einsum('jbh,jbhpn->bhpn', jnp.exp(log_before), grad_all, precision=HI...  85 us
    dot_general x1, matrix products, link_states(): jnp.einsum('jbh,jbhpn->bhpn', w_right, grad_all, precision=HIGH_PREC, pre...  84.6 us
    dot_general x1, matrix products, link_states(): jnp.einsum('jbh,jbhpn->bhpn', w_left, state_all, precision=HIGH_PREC, pre...  83.2 us
    dot_general x9, matrix products, chunk_step(): jnp.einsum('bhpn,btn->bthp', carry_state, c_blk, precision=HIGH_PREC, pre...  52.6 us
    dot_general x9, matrix products, chunk_step(): jnp.einsum('bsh,bshp,bsn->bhpn', tail_decay, u_blk, b_blk, precision=HIGH...  49.8 us
  transfers between devices with their start and end apart: 2, of which 2 were waited for; matrix products, arithmetic and copies ran while one was open for 17% of the time, Pallas kernels for 0%

commit v1 on v0

v1 whole, which is shorter than its diff:
```python
import functools
import jax
import jax.numpy as jnp
from jax import lax
from jax.sharding import PartitionSpec as P
from jax.experimental import pallas as pl
from jax.experimental.pallas import tpu as pltpu

AXIS = 'cp'
HEADS, HD, N = 64, 64, 128
GH = 8
GR = GH * HD
T = 128
LOG2E = 1.4426950408889634
F32, BF16 = jnp.float32, jnp.bfloat16
MESH = pl.DeviceIdType.MESH


def mm(a, b):
    return lax.dot_general(a, b, (((1,), (0,)), ((), ())), preferred_element_type=F32)


def mm_nt(a, b):
    return lax.dot_general(a, b, (((1,), (1,)), ((), ())), preferred_element_type=F32)


def mm_tn(a, b):
    return lax.dot_general(a, b, (((0,), (0,)), ((), ())), preferred_element_type=F32)


def split2(v):
    hi = v.astype(BF16)
    return hi, (v - hi.astype(F32)).astype(BF16)


def split3(v):
    hi = v.astype(BF16)
    r = v - hi.astype(F32)
    mid = r.astype(BF16)
    return hi, mid, (r - mid.astype(F32)).astype(BF16)


def dot_tri(v, tri):
    hi, mid, lo = split3(v)
    return mm(hi, tri) + mm(mid, tri) + mm(lo, tri)


def tri_mask(upper):
    r = lax.broadcasted_iota(jnp.int32, (T, T), 0)
    c = lax.broadcasted_iota(jnp.int32, (T, T), 1)
    keep = (r <= c) if upper else (r >= c)
    return jnp.where(keep, 1.0, 0.0)


def summary_kernel(nb, x_ref, dy_ref, dt_ref, rate_ref, b_ref, c_ref,
                   s_ref, ds_ref, ld_ref, cum_ref, xw, yw):
    tri = tri_mask(True).astype(BF16)
    dt = dt_ref[...]
    a = dt * rate_ref[:, 0:1]
    cums, tots = [], []
    for i in range(nb):
        cum = dot_tri(a[:, i * T:(i + 1) * T], tri)
        cum_ref[:, i * T:(i + 1) * T] = cum
        cums.append(cum)
        tots.append(cum[:, T - 1:T])
    before = [jnp.zeros_like(tots[0])]
    for i in range(nb):
        before.append(before[-1] + tots[i])
    after = [jnp.zeros_like(tots[0])]
    for i in reversed(range(1, nb)):
        after.append(after[-1] + tots[i])
    after = after[::-1]
    ld_ref[...] = jnp.broadcast_to(before[nb], (GH, T))
    for i in range(nb):
        w_in = dt[:, i * T:(i + 1) * T] * jnp.exp2((tots[i] - cums[i]) + after[i])
        w_out = jnp.exp2(cums[i] + before[i])
        lo_off = nb * T + i * T
        for j in range(GH):
            rows = slice(j * HD, (j + 1) * HD)
            hi, lo = split2(x_ref[rows, i * T:(i + 1) * T].astype(F32) * w_in[j:j + 1, :])
            xw[rows, i * T:(i + 1) * T] = hi
            xw[rows, lo_off:lo_off + T] = lo
            hi, lo = split2(dy_ref[rows, i * T:(i + 1) * T].astype(F32) * w_out[j:j + 1, :])
            yw[rows, i * T:(i + 1) * T] = hi
            yw[rows, lo_off:lo_off + T] = lo
    bb = b_ref[...]
    cc = c_ref[...]
    s_ref[...] = mm(xw[...], jnp.concatenate([bb, bb], axis=0))
    ds_ref[...] = mm(yw[...], jnp.concatenate([cc, cc], axis=0))


def summaries(x_t, dy_t, dt_t, rate, b, c):
    seq = x_t.shape[1]
    nb = seq // T
    rows = x_t.shape[0]
    big = pl.BlockSpec((GR, seq), lambda g: (g, 0))
    head = pl.BlockSpec((GH, seq), lambda g: (g, 0))
    hd1 = pl.BlockSpec((GH, T), lambda g: (g, 0))
    full = pl.BlockSpec((seq, N), lambda g: (0, 0))
    st = pl.BlockSpec((GR, N), lambda g: (g, 0))
    return pl.pallas_call(
        functools.partial(summary_kernel, nb),
        grid=(rows // GR,),
        in_specs=[big, big, head, hd1, full, full],
        out_specs=[st, st, hd1, head],
        out_shape=[jax.ShapeDtypeStruct((rows, N), F32), jax.ShapeDtypeStruct((rows, N), F32),
                   jax.ShapeDtypeStruct((rows // HD, T), F32), jax.ShapeDtypeStruct((rows // HD, seq), F32)],
        scratch_shapes=[pltpu.VMEM((GR, 2 * seq), BF16), pltpu.VMEM((GR, 2 * seq), BF16)],
        compiler_params=pltpu.CompilerParams(dimension_semantics=("arbitrary",)),
        name="summary",
    )(x_t, dy_t, dt_t, rate, b, c)


def main_kernel(nb, ng, x_ref, dy_ref, dt_ref, cum_ref, rate_ref, skip_ref, s0_ref, dse_ref, b_ref, c_ref,
                dx_ref, ddt_ref, dal_ref, dsk_ref, db_ref, dc_ref,
                gram, dgram, db_acc, dc_acc, s_cur, ds_cur, xw, yw, d_u, y_in, dcum, xdu):
    g = pl.program_id(0)

    @pl.when(g == 0)
    def _():
        low = tri_mask(False)
        for i in range(nb):
            tok = slice(i * T, (i + 1) * T)
            gram[i] = mm_nt(c_ref[tok, :], b_ref[tok, :]) * low
            dgram[i] = jnp.zeros((T, T), F32)
        db_acc[...] = jnp.zeros_like(db_acc)
        dc_acc[...] = jnp.zeros_like(dc_acc)

    ds_cur[...] = dse_ref[...]
    s_cur[...] = s0_ref[...]

    @pl.loop(0, nb)
    def _(it):
        i = nb - 1 - it
        tok = pl.ds(pl.multiple_of(i * T, T), T)
        cum = cum_ref[:, tok]
        tot = cum[:, T - 1:T]
        e_in = jnp.exp2(tot - cum)
        e_out = jnp.exp2(cum)
        w_in = dt_ref[:, tok] * e_in
        for j in range(GH):
            rows = slice(j * HD, (j + 1) * HD)
            hi, lo = split2(x_ref[rows, tok].astype(F32) * w_in[j:j + 1, :])
            xw[i, rows, 0:T] = hi
            xw[i, rows, T:2 * T] = lo
            hi, lo = split2(dy_ref[rows, tok].astype(F32) * e_out[j:j + 1, :])
            yw[i, rows, 0:T] = hi
            yw[i, rows, T:2 * T] = lo
        ds_hi, ds_lo = split2(ds_cur[...])
        bb = b_ref[tok, :]
        cc = c_ref[tok, :]
        inter = mm_nt(jnp.concatenate([ds_hi, ds_lo], axis=1), jnp.concatenate([bb, bb], axis=1))
        x_hi = xw[i, :, 0:T]
        db_acc[tok, :] += mm_tn(jnp.concatenate([x_hi, xw[i, :, T:2 * T], x_hi], axis=0),
                                jnp.concatenate([ds_hi, ds_hi, ds_lo], axis=0))
        upd = mm(yw[i], jnp.concatenate([cc, cc], axis=0))
        e_tot = jnp.exp2(tot)
        for j in range(GH):
            rows = slice(j * HD, (j + 1) * HD)
            d_u[rows, tok] = inter[rows, :] * e_in[j:j + 1, :]
            ds_cur[rows, :] = ds_cur[rows, :] * e_tot[j:j + 1, :] + upd[rows, :]

    @pl.loop(0, nb)
    def _(i):
        tok = pl.ds(pl.multiple_of(i * T, T), T)
        cum = cum_ref[:, tok]
        tot = cum[:, T - 1:T]
        e_tot = jnp.exp2(tot)
        e_out = jnp.exp2(cum)
        dt = dt_ref[:, tok]
        s_hi, s_lo = split2(s_cur[...])
        bb = b_ref[tok, :]
        cc = c_ref[tok, :]
        y_in[...] = mm_nt(jnp.concatenate([s_hi, s_lo], axis=1), jnp.concatenate([cc, cc], axis=1))
        y_hi = yw[i, :, 0:T]
        dc_acc[tok, :] += mm_tn(jnp.concatenate([y_hi, yw[i, :, T:2 * T], y_hi], axis=0),
                                jnp.concatenate([s_hi, s_hi, s_lo], axis=0))
        upd = mm(xw[i], jnp.concatenate([bb, bb], axis=0))
        for j in range(GH):
            rows = slice(j * HD, (j + 1) * HD)
            s_cur[rows, :] = s_cur[rows, :] * e_tot[j:j + 1, :] + upd[rows, :]
        cum_c = jnp.transpose(cum)
        g_i = gram[i]
        for j in range(GH):
            rows = slice(j * HD, (j + 1) * HD)
            row = slice(j, j + 1)
            xb = x_ref[rows, tok]
            yb = dy_ref[rows, tok]
            xf = xb.astype(F32)
            yf = yb.astype(F32)
            dtr = dt[row, :]
            u_hi, u_lo = split2(xf * dtr)
            pair = mm_tn(jnp.concatenate([yb, yb], axis=0), jnp.concatenate([u_hi, u_lo], axis=0))
            lam = jnp.exp2(jnp.minimum(cum_c[:, j:j + 1] - cum[row, :], 0.0))
            dgram[i] += lam * pair
            m_hi, m_lo = split2(lam * g_i)
            du_b = mm(jnp.concatenate([yb, yb], axis=1), jnp.concatenate([m_hi, m_lo], axis=0))
            zero = jnp.zeros_like(u_lo)
            y2 = mm_nt(jnp.concatenate([jnp.concatenate([u_hi, u_hi], axis=1),
                                        jnp.concatenate([u_lo, zero], axis=1)], axis=0),
                       jnp.concatenate([m_hi, m_lo], axis=1))
            y = (y2[0:HD] + y2[HD:2 * HD]) + e_out[row, :] * y_in[rows, :]
            du = d_u[rows, tok] + du_b
            dx_ref[rows, tok] = (dtr * du + skip_ref[row, :] * yf).astype(BF16)
            xd = jnp.sum(xf * du, axis=0, keepdims=True)
            xdu[row, tok] = xd
            dcum[row, tok] = jnp.sum(yf * y, axis=0, keepdims=True) - dtr * xd
            sk = jnp.sum(xf * yf, axis=0, keepdims=True)

            @pl.when(i == 0)
            def _():
                dsk_ref[row, :] = sk

            @pl.when(i != 0)
            def _():
                dsk_ref[row, :] += sk

    for j in range(GH):
        rows = slice(j * HD, (j + 1) * HD)
        dal_ref[j:j + 1, :] = jnp.sum(dse_ref[rows, :] * s_cur[rows, :], axis=0, keepdims=True)
    run = jnp.sum(dal_ref[...], axis=1, keepdims=True)
    rate = rate_ref[:, T - 1:T] * (1.0 / LOG2E)
    low = tri_mask(False).astype(BF16)
    total = jnp.zeros((GH, T), F32)
    for i in reversed(range(nb)):
        tok = slice(i * T, (i + 1) * T)
        da = dot_tri(dcum[:, tok], low) + run
        run = da[:, 0:1]
        da = da * rate
        ddt_ref[:, tok] = xdu[:, tok] + da
        total = total + dt_ref[:, tok] * da
    dal_ref[...] = jnp.broadcast_to(jnp.sum(total, axis=1, keepdims=True), (GH, T))
    dsk_ref[...] = jnp.broadcast_to(jnp.sum(dsk_ref[...], axis=1, keepdims=True), (GH, T))

    @pl.when(g == ng - 1)
    def _():
        low_f = tri_mask(False)
        for i in range(nb):
            tok = slice(i * T, (i + 1) * T)
            bb = b_ref[tok, :]
            cc = c_ref[tok, :]
            hi, lo = split2(dgram[i] * low_f)
            dc_ref[tok, :] = (dc_acc[tok, :] + (mm(hi, bb) + mm(lo, bb))).astype(BF16)
            db_ref[tok, :] = (db_acc[tok, :] + (mm_tn(hi, cc) + mm_tn(lo, cc))).astype(BF16)


def main_grads(x_t, dy_t, dt_t, cum, rate, skip, s0, dse, b, c):
    rows, seq = x_t.shape
    nb, ng = seq // T, rows // GR
    big = pl.BlockSpec((GR, seq), lambda g: (g, 0))
    head = pl.BlockSpec((GH, seq), lambda g: (g, 0))
    hd1 = pl.BlockSpec((GH, T), lambda g: (g, 0))
    full = pl.BlockSpec((seq, N), lambda g: (0, 0))
    st = pl.BlockSpec((GR, N), lambda g: (g, 0))
    sd = jax.ShapeDtypeStruct
    return pl.pallas_call(
        functools.partial(main_kernel, nb, ng),
        grid=(ng,),
        in_specs=[big, big, head, head, hd1, hd1, st, st, full, full],
        out_specs=[big, head, hd1, hd1, full, full],
        out_shape=[sd((rows, seq), BF16), sd((rows // HD, seq), F32), sd((rows // HD, T), F32),
                   sd((rows // HD, T), F32), sd((seq, N), BF16), sd((seq, N), BF16)],
        scratch_shapes=[pltpu.VMEM((nb, T, T), F32), pltpu.VMEM((nb, T, T), F32),
                        pltpu.VMEM((seq, N), F32), pltpu.VMEM((seq, N), F32),
                        pltpu.VMEM((GR, N), F32), pltpu.VMEM((GR, N), F32),
                        pltpu.VMEM((nb, GR, 2 * T), BF16), pltpu.VMEM((nb, GR, 2 * T), BF16),
                        pltpu.VMEM((GR, seq), F32), pltpu.VMEM((GR, T), F32),
                        pltpu.VMEM((GH, seq), F32), pltpu.VMEM((GH, seq), F32)],
        compiler_params=pltpu.CompilerParams(dimension_semantics=("arbitrary",)),
        name="main_grads",
    )(x_t, dy_t, dt_t, cum, rate, skip, s0, dse, b, c)


def link_kernel(sp, dsp, ld, s_init, ds_last, start, end, first,
                r_s, r_ds, r_ld, c_s, c_ds, c_ld, p_s, p_ds, p_ld, t_s, t_ds, t_ld, z_b, z_ld,
                b_s, b_ds, a_s, a_ds, o_s, o_ds, f_own, f_all,
                send0, recv0, send1, recv1, send2, recv2, send3, recv3, send4, recv4, send5, recv5):
    me = lax.axis_index(AXIS)
    core = lax.rem(me, 2)
    chip = lax.rem(me // 2, 4)
    z = me // 8
    partner = z * 8 + chip * 2 + (1 - core)

    def at_chip(c):
        return z * 8 + c * 2 + core

    def at_z(zz):
        return zz * 8 + chip * 2 + core

    peers = [partner] + [at_chip(lax.rem(chip + r, 4)) for r in (1, 2, 3)] + [at_z(lax.rem(z + r, 4)) for r in (1, 2, 3)]
    barrier = pltpu.get_barrier_semaphore()
    for p in peers:
        pl.semaphore_signal(barrier, inc=1, device_id=(p,), device_id_type=MESH)
    pl.semaphore_wait(barrier, len(peers))

    def rcopy(src, dst, ssem, rsem, dev):
        return pltpu.make_async_remote_copy(src_ref=src, dst_ref=dst, send_sem=ssem, recv_sem=rsem,
                                            device_id=(dev,), device_id_type=MESH)

    h0 = core * 32
    o0 = (1 - core) * 32
    st0 = [rcopy(sp.at[pl.ds(o0, 32)], r_s, send0.at[0], recv0.at[0], partner),
           rcopy(dsp.at[pl.ds(o0, 32)], r_ds, send0.at[1], recv0.at[1], partner),
           rcopy(ld, r_ld, send0.at[2], recv0.at[2], partner)]
    for cp in st0:
        cp.start()
    for cp in st0:
        cp.wait()

    @pl.loop(0, 32)
    def _(h):
        hh = h0 + h
        own = jnp.exp2(ld[pl.ds(hh, 1), :])
        oth = jnp.exp2(r_ld[pl.ds(hh, 1), :])
        c_ld[pl.ds(h, 1), :] = ld[pl.ds(hh, 1), :] + r_ld[pl.ds(hh, 1), :]

        @pl.when(core == 0)
        def _():
            c_s[h] = sp[hh] * oth + r_s[h]
            c_ds[h] = dsp[hh] + own * r_ds[h]

        @pl.when(core == 1)
        def _():
            c_s[h] = r_s[h] * own + sp[hh]
            c_ds[h] = r_ds[h] + oth * dsp[hh]

    def copies1(c_dst, c_slot):
        part = pl.ds(c_dst * 8, 8)
        dev = at_chip(c_dst)
        return [rcopy(c_s.at[part], p_s.at[c_slot], send1.at[0, c_dst], recv1.at[0, c_slot], dev),
                rcopy(c_ds.at[part], p_ds.at[c_slot], send1.at[1, c_dst], recv1.at[1, c_slot], dev),
                rcopy(c_ld.at[part], p_ld.at[c_slot], send1.at[2, c_dst], recv1.at[2, c_slot], dev)]

    for r in (2, 1, 3):
        for cp in copies1(lax.rem(chip + r, 4), chip):
            cp.start()

    @pl.loop(0, 8)
    def _(h):
        p_s[chip, h] = c_s[chip * 8 + h]
        p_ds[chip, h] = c_ds[chip * 8 + h]
    p_ld[chip] = c_ld[pl.ds(pl.multiple_of(chip * 8, 8), 8), :]
    for r in (1, 2, 3):
        other = lax.rem(chip + r, 4)
        for cp in copies1(other, other):
            cp.wait_recv()

    t_ld[...] = p_ld[0] + p_ld[1] + p_ld[2] + p_ld[3]

    @pl.loop(0, 8)
    def _(h):
        d = [jnp.exp2(p_ld[c, pl.ds(h, 1), :]) for c in range(4)]
        acc = p_s[0, h]
        for c in (1, 2, 3):
            acc = acc * d[c] + p_s[c, h]
        t_s[h] = acc
        acc = p_ds[3, h]
        for c in (2, 1, 0):
            acc = acc * d[c] + p_ds[c, h]
        t_ds[h] = acc

    def copies2(z_dst, z_slot):
        return (rcopy(t_s, z_b.at[z_slot], send2.at[0, z_dst], recv2.at[0, z_slot], at_z(z_dst)),
                rcopy(t_ds, z_b.at[z_slot], send2.at[0, z_dst], recv2.at[0, z_slot], at_z(z_dst)),
                rcopy(t_ld, z_ld.at[z_slot], send2.at[1, z_dst], recv2.at[1, z_slot], at_z(z_dst)))

    for r in (1, 2, 3):
        zz = lax.rem(z + r, 4)
        right, left, dec = copies2(zz, z)

        @pl.when(zz > z)
        def _():
            right.start()

        @pl.when(zz < z)
        def _():
            left.start()
        dec.start()
    for r in (1, 2, 3):
        zz = lax.rem(z + r, 4)
        right, left, dec = copies2(zz, zz)
        right.wait_recv()
        dec.wait_recv()

    part8 = h0 + chip * 8

    @pl.loop(0, 8)
    def _(h):
        b_s[0, h] = s_init[part8 + h]
        b_ds[3, h] = ds_last[part8 + h]
        for zz in range(4):
            @pl.when(zz < z)
            def _():
                b_s[0, h] = b_s[0, h] * jnp.exp2(z_ld[zz, pl.ds(h, 1), :]) + z_b[zz, h]
        for zz in (3, 2, 1):
            @pl.when(zz > z)
            def _():
                b_ds[3, h] = b_ds[3, h] * jnp.exp2(z_ld[zz, pl.ds(h, 1), :]) + z_b[zz, h]
        d = [jnp.exp2(p_ld[c, pl.ds(h, 1), :]) for c in range(4)]
        acc = b_s[0, h]
        for c in (0, 1, 2):
            acc = acc * d[c] + p_s[c, h]
            b_s[c + 1, h] = acc
        acc = b_ds[3, h]
        for c in (3, 2, 1):
            acc = acc * d[c] + p_ds[c, h]
            b_ds[c - 1, h] = acc
        f_own[h] = acc * d[0] + p_ds[0, h]

    def copies3(c_dst, c_slot):
        dev = at_chip(c_dst)
        return [rcopy(b_s.at[c_dst], a_s.at[c_slot], send3.at[0, c_dst], recv3.at[0, c_slot], dev),
                rcopy(b_ds.at[c_dst], a_ds.at[c_slot], send3.at[1, c_dst], recv3.at[1, c_slot], dev)]

    for r in (2, 1, 3):
        for cp in copies3(lax.rem(chip + r, 4), chip):
            cp.start()

    def copy_f(zz):
        return rcopy(f_own, f_all.at[chip], send5.at[0, zz], recv5.at[0, chip], at_z(zz))

    @pl.when(z == 0)
    def _():
        for zz in (1, 2, 3):
            copy_f(zz).start()

        @pl.loop(0, 8)
        def _(h):
            f_all[chip, h] = f_own[h]

    @pl.loop(0, 8)
    def _(h):
        a_s[chip, h] = b_s[chip, h]
        a_ds[chip, h] = b_ds[chip, h]

    for r in (1, 2, 3):
        other = lax.rem(chip + r, 4)
        for cp in copies3(other, other):
            cp.wait_recv()

    def pair(h, c, hc):
        hh = h0 + h
        own = jnp.exp2(ld[pl.ds(hh, 1), :])
        oth = jnp.exp2(r_ld[pl.ds(hh, 1), :])

        @pl.when(core == 0)
        def _():
            start[hh] = a_s[c, hc]
            end[hh] = r_ds[h] + oth * a_ds[c, hc]
            o_s[h] = own * a_s[c, hc] + sp[hh]
            o_ds[h] = a_ds[c, hc]

        @pl.when(core == 1)
        def _():
            start[hh] = oth * a_s[c, hc] + r_s[h]
            end[hh] = a_ds[c, hc]
            o_s[h] = a_s[c, hc]
            o_ds[h] = dsp[hh] + own * a_ds[c, hc]

    for c in range(4):
        @pl.loop(0, 8)
        def _(hc):
            pair(c * 8 + hc, c, hc)

    mine = pl.ds(h0, 32)
    st4 = [rcopy(o_s, start.at[mine], send4.at[0], recv4.at[0], partner),
           rcopy(o_ds, end.at[mine], send4.at[1], recv4.at[1], partner)]
    for cp in st4:
        cp.start()

    @pl.when(z > 0)
    def _():
        copy_f(z).wait_recv()

    def copies5(c_dst, c_slot):
        return rcopy(f_all.at[chip], f_all.at[c_slot], send5.at[1, c_dst], recv5.at[1, c_slot], at_chip(c_dst))

    for r in (2, 1, 3):
        copies5(lax.rem(chip + r, 4), chip).start()
    for r in (1, 2, 3):
        other = lax.rem(chip + r, 4)
        copies5(other, other).wait_recv()

    for c in range(4):
        @pl.loop(0, 8)
        def _(hc):
            first[h0 + c * 8 + hc] = f_all[c, hc]
    last = [rcopy(f_all.at[c], first.at[pl.ds(h0 + c * 8, 8)], send5.at[2, c], recv5.at[2, c], partner) for c in range(4)]
    for cp in last:
        cp.start()
    for cp in last:
        cp.wait_recv()
    for cp in st4:
        cp.wait()
    for cp in last:
        cp.wait_send()
    for r in (1, 2, 3):
        other = lax.rem(chip + r, 4)
        for cp in copies1(other, chip) + copies3(other, chip) + [copies5(other, chip)]:
            cp.wait_send()
        zz = lax.rem(z + r, 4)
        right, left, dec = copies2(zz, z)
        right.wait_send()
        dec.wait_send()

    @pl.when(z == 0)
    def _():
        for zz in (1, 2, 3):
            copy_f(zz).wait_send()


def link_ranges(sp, dsp, ld, s_init, ds_last):
    vm = pl.BlockSpec(memory_space=pltpu.VMEM)
    st = (HD, N)
    V = pltpu.VMEM
    D = pltpu.SemaphoreType.DMA
    full = jax.ShapeDtypeStruct((HEADS,) + st, F32)
    return pl.pallas_call(
        link_kernel,
        in_specs=[vm] * 5,
        out_specs=[vm] * 3,
        out_shape=[full, full, full],
        scratch_shapes=[V((32,) + st, F32), V((32,) + st, F32), V((HEADS, N), F32),
                        V((32,) + st, F32), V((32,) + st, F32), V((32, N), F32),
                        V((4, 8) + st, F32), V((4, 8) + st, F32), V((4, 8, N), F32),
                        V((8,) + st, F32), V((8,) + st, F32), V((8, N), F32),
                        V((4, 8) + st, F32), V((4, 8, N), F32),
                        V((4, 8) + st, F32), V((4, 8) + st, F32),
                        V((4, 8) + st, F32), V((4, 8) + st, F32),
                        V((32,) + st, F32), V((32,) + st, F32),
                        V((8,) + st, F32), V((4, 8) + st, F32),
                        D((3,)), D((3,)), D((3, 4)), D((3, 4)), D((2, 4)), D((2, 4)),
                        D((2, 4)), D((2, 4)), D((2,)), D((2,)), D((3, 4)), D((3, 4))],
        compiler_params=pltpu.CompilerParams(collective_id=0, has_side_effects=True),
        name="link_ranges",
    )(sp, dsp, ld, s_init, ds_last)


def solution(mesh):
    tok4 = P(None, AXIS, None, None)
    tok3 = P(None, AXIS, None)

    def device_step(x_loc, dt_loc, a_log, b_loc, c_loc, d_skip, s_init, dy_loc, ds_last):
        seq = x_loc.shape[1]
        x_t = x_loc[0].transpose(1, 2, 0).reshape(HEADS * HD, seq)
        dy_t = dy_loc[0].transpose(1, 2, 0).reshape(HEADS * HD, seq)
        dt_t = dt_loc[0].T
        rate = jnp.broadcast_to((-jnp.exp(a_log) * LOG2E)[:, None], (HEADS, T))
        skip = jnp.broadcast_to(d_skip[:, None], (HEADS, T))
        b, c = b_loc[0], c_loc[0]
        sp, dsp, ld, cum = summaries(x_t, dy_t, dt_t, rate, b, c)
        st = (HEADS, HD, N)
        start, end, first = link_ranges(sp.reshape(st), dsp.reshape(st), ld, s_init[0], ds_last[0])
        dx, ddt, dal, dsk, db, dc = main_grads(x_t, dy_t, dt_t, cum, rate, skip, start.reshape(HEADS * HD, N),
                                               end.reshape(HEADS * HD, N), b, c)
        grad_x = dx.reshape(HEADS, HD, seq).transpose(2, 0, 1)[None]
        grad_alog, grad_skip = lax.psum((dal[:, 0], dsk[:, 0]), AXIS)
        return grad_x, ddt.T[None], db[None], dc[None], first[None], grad_alog, grad_skip

    return jax.shard_map(device_step, mesh=mesh,
                         in_specs=(tok4, tok3, P(), tok3, tok3, P(), P(), tok4, P()),
                         out_specs=(tok4, tok3, tok3, tok3, P(), P(), P()),
                         check_vma=False)
```

time: 1290 us -> 322 us (0.25)
  matrix products: 519 us -> 0 us
  waiting for transfers between devices: 452 us -> 0 us
  Pallas kernels: 0 us -> 270 us
  local copies, waits for them, and re-layouts: 153 us -> 4.21 us
  other arithmetic: 39.3 us -> 0.66 us
  blocking collectives: 82.2 us -> 45.9 us
  loops' own time: 25.1 us -> 0 us
  between operations: 14.6 us -> 0.67 us
    dot_general x38 -> x0, matrix products: 519 us -> none  [the longest x6 141 us: chunk_step(): jnp.einsum('btsh,bshp->bthp', mix_mat, u_blk, precision=HIGH_PREC, prefer...]
    all_gather x2 -> x0, waiting for transfers between devices: 452 us -> none  [the longest x1 265 us: device_step(): grad_all = lax.all_gather(grad_part, AXIS)]
    pallas_call x0 -> x3, Pallas kernels: none -> 270 us  [the longest x1 156 us: main_grads(): pl.pallas_call(functools.partial(main_kernel, nb, ng), grid=(ng,), in_spe...]
    squeeze x15 -> x0, local copies, waits for them, and re-layouts: 72.9 us -> none  [the longest x3 37.8 us: ssd_forward(): final_state, y_blocks = lax.scan(jax.checkpoint(span_step), s_init, seq_in)]
    all_gather x1 -> x0, blocking collectives: 43.8 us -> none  [device_step(): logdec_all = lax.all_gather(log_part, AXIS)]
    another operation x2 -> x0, loops' own time: 25.1 us -> none  [span_step(): return lax.scan(inner_step, carry_state, span_in)]
    dynamic_slice x3 -> x0, local copies, waits for them, and re-layouts: 22.1 us -> none  [span_step(): return lax.scan(inner_step, carry_state, span_in)]
    dynamic_update_slice x6 -> x0, local copies, waits for them, and re-layouts: 16.6 us -> none  [span_step(): return lax.scan(inner_step, carry_state, span_in)]
  transfers between devices with their start and end apart: 2 -> 0, of which waited for: 2 -> 0; matrix products, arithmetic and copies ran while one was open for 17% -> 0% of each run, Pallas kernels for 0% -> 0%
where the time goes in v1:
time: 322 us
  Pallas kernels  270 us (84%)
  blocking collectives  45.9 us (14%)
  local copies, waits for them, and re-layouts  4.21 us (1%)
    pallas_call x1, Pallas kernels, main_grads(): pl.pallas_call(functools.partial(main_kernel, nb, ng), grid=(ng,), in_spe...  156 us
    pallas_call x1, Pallas kernels, link_ranges(): pl.pallas_call(link_kernel, in_specs=[vm] * 5, out_specs=[vm] * 3, out_sh...  100 us
    psum x1, blocking collectives, device_step(): grad_alog, grad_skip = lax.psum((dal[:, 0], dsk[:, 0]), AXIS)  45.9 us
    pallas_call x1, Pallas kernels, summaries(): pl.pallas_call(functools.partial(summary_kernel, nb), grid=(rows // GR,),...  14.5 us

profile of v1, /device:TPU:0, one launch (start us, length us, event | category | flops | bytes accessed | tf_op | source)
XLA Modules:
  0.0 321.6 jit_solution(15057975625516824231)
XLA Ops:
  0.6 0.7 negate_multiply_fusion
  1.3 0.7 broadcast_in_dim.27.rate_ref
  2.0 1.3 broadcast_in_dim.28.skip_ref
  3.3 14.5 %summary.1 = (f32[4096,128]{1,0:T(8,128)}, f32[4096,128]{1,0:T(8,128)}, f32[64,128]{1,0:T(8,128)}, f32[64,768]{1,0:T(8,128)}) custom-call(bf16[4096,768]{1,0:T(8,128)(2,1)} %bitcast.32, bf16[4096,768]{1,0:T(8,128)(2,1)} %bitcast.34, f32[64,768]{1,0:T(8,128)} %bitcast.43, f32[64,128]{1,0:T(8,128)} %broadcast_in_dim.27.rate_ref, bf16[768,128]{1,0:T(8,128)(2,1)} %bitcast.45, ...), custom_call_target="tpu_custom_call" | custom-call | tf_op jit(solution)/shard_map/summary/pallas_call | solution.py:101
  17.8 100.0 %link_ranges.1 = (f32[64,64,128]{2,1,0:T(8,128)}, f32[64,64,128]{2,1,0:T(8,128)}, f32[64,64,128]{2,1,0:T(8,128)}) custom-call(f32[64,64,128]{2,1,0:T(8,128)} %bitcast.41, f32[64,64,128]{2,1,0:T(8,128)} %bitcast.42, f32[64,128]{1,0:T(8,128)} %get-tuple-element.23.ld, f32[64,64,128]{2,1,0:T(8,128)} %bitcast.39, f32[64,64,128]{2,1,0:T(8,128)} %bitcast.40), custom_call_target="tpu_custom_call" | custom-call | tf_op jit(solution)/shard_map/link_ranges/pallas_call | solution.py:518
  117.8 0.0 copy-start
  117.8 155.7 %main_grads.1 = (bf16[4096,768]{1,0:T(8,128)(2,1)}, f32[64,768]{1,0:T(8,128)}, f32[64,128]{1,0:T(8,128)}, f32[64,128]{1,0:T(8,128)}, bf16[768,128]{1,0:T(8,128)(2,1)}, /*index=5*/bf16[768,128]{1,0:T(8,128)(2,1)}) custom-call(bf16[4096,768]{1,0:T(8,128)(2,1)} %bitcast.33, bf16[4096,768]{1,0:T(8,128)(2,1)} %bitcast.35, f32[64,768]{1,0:T(8,128)} %bitcast.44, ...), custom_call_target="tpu_custom_call" | custom-call | tf_op jit(solution)/shard_map/main_grads/pallas_call | solution.py:256
  273.5 0.9 slice_reduce_fusion
  274.4 45.9 %all-reduce = (f32[64]{0:T(128)}, f32[64]{0:T(128)}) all-reduce(f32[64]{0:T(128)S(1)} %get-tuple-element.36, f32[64]{0:T(128)S(1)} %get-tuple-element.35), channel_id=1, replica_groups=mesh['cp'=32] {'cp'}, use_global_device_ids=true, to_apply=%region_0.0 | all-reduce | flops 128 | bytes 1024 | tf_op jit(solution)/shard_map/psum | solution.py:557
  320.3 0.0 copy-done
  320.3 1.3 copy.17
Async XLA Ops:
  117.8 202.5 %copy-start = (f32[64,64,128]{2,1,0:T(8,128)S(1)}, f32[64,64,128]{2,1,0:T(8,128)}, u32[]{:S(2)}) copy-start(f32[64,64,128]{2,1,0:T(8,128)} %get-tuple-element.30) | copy-start | bytes 6291460

commit v2 on v0

v2 whole, which is shorter than its diff:
```python
import functools
import jax
import jax.numpy as jnp
from jax import lax
from jax.sharding import PartitionSpec as P
from jax.experimental import pallas as pl
from jax.experimental.pallas import tpu as pltpu

AXIS = 'cp'
HEADS, HD, N = 64, 64, 128
GH = 8
GR = GH * HD
T = 128
PIECE, SHARE, OWN, CHIPS, PLANES, QS = 32, 16, 4, 4, 4, 2
ALL_CHIPS = range(CHIPS)
LOG2E = 1.4426950408889634
F32, BF16 = jnp.float32, jnp.bfloat16
MESH = pl.DeviceIdType.MESH


def mm(a, b):
    return lax.dot_general(a, b, (((1,), (0,)), ((), ())), preferred_element_type=F32)


def mm_nt(a, b):
    return lax.dot_general(a, b, (((1,), (1,)), ((), ())), preferred_element_type=F32)


def mm_tn(a, b):
    return lax.dot_general(a, b, (((0,), (0,)), ((), ())), preferred_element_type=F32)


def cat0(*parts):
    return jnp.concatenate(parts, axis=0)


def cat1(*parts):
    return jnp.concatenate(parts, axis=1)


def sum0(v):
    return jnp.sum(v, axis=0, keepdims=True)


def sum1(v):
    return jnp.sum(v, axis=1, keepdims=True)


def blk(i, size):
    return slice(i * size, (i + 1) * size)


def row(v, j):
    return v[blk(j, 1), :]


def last_col(v):
    return v[:, T - 1:T]


def split2(v):
    hi = v.astype(BF16)
    return hi, (v - hi.astype(F32)).astype(BF16)


def split3(v):
    hi = v.astype(BF16)
    r = v - hi.astype(F32)
    mid = r.astype(BF16)
    return hi, mid, (r - mid.astype(F32)).astype(BF16)


def dot_tri(v, tri):
    hi, mid, lo = split3(v)
    return mm(hi, tri) + mm(mid, tri) + mm(lo, tri)


def tri_mask(upper):
    r = lax.broadcasted_iota(jnp.int32, (T, T), 0)
    c = lax.broadcasted_iota(jnp.int32, (T, T), 1)
    keep = (r <= c) if upper else (r >= c)
    return jnp.where(keep, 1.0, 0.0)


def neighbours():
    me = lax.axis_index(AXIS)
    core = lax.rem(me, 2)
    chip = lax.rem(me // 2, CHIPS)
    z = me // (2 * CHIPS)
    partner = me + 1 - 2 * core
    chips = [lax.rem(chip + r, CHIPS) for r in (2, 1, 3)]
    planes = [lax.rem(z + r, PLANES) for r in (1, 2, 3)]

    def at_chip(c):
        return me + 2 * (c - chip)

    def at_z(zz):
        return me + 2 * CHIPS * (zz - z)

    return core, chip, z, partner, chips, planes, at_chip, at_z


def greet(partner, chips, planes, at_chip, at_z):
    barrier = pltpu.get_barrier_semaphore()
    for p in [partner] + [at_chip(c) for c in chips] + [at_z(zz) for zz in planes]:
        pl.semaphore_signal(barrier, inc=1, device_id=(p,), device_id_type=MESH)


def met(chips, planes):
    pl.semaphore_wait(pltpu.get_barrier_semaphore(), 1 + len(chips) + len(planes))


def rcopy(src, dst, ssem, rsem, dev):
    return pltpu.make_async_remote_copy(src_ref=src, dst_ref=dst, send_sem=ssem, recv_sem=rsem,
                                        device_id=(dev,), device_id_type=MESH)


def each(copies, act):
    for cp in copies:
        getattr(cp, act)()


def link_steps(ng, sp, dsp, ld, s_init, ds_last, start, end, first, sp_out,
               r_s, r_ds, r_ld, c_s, c_ds, c_ld, p_s, p_ds, p_ld, t_s, t_ds, t_ld, z_b, z_ld,
               b_s, b_ds, a_s, a_ds, n_s, n_ds, o_s, o_ds, f_own, f_all,
               send0, recv0, send1, recv1, send2, recv2, send3, recv3, send4, recv4, send5, recv5, loc):
    core, chip, z, partner, chips, planes, at_chip, at_z = neighbours()
    mine, theirs = core * SHARE, (1 - core) * SHARE

    def hello():
        greet(partner, chips, planes, at_chip, at_z)

    def own_loads(q):
        part = pl.ds(q * PIECE + mine + chip * OWN, OWN)
        return [pltpu.make_async_copy(s_init.at[part], b_s.at[q, 0], loc.at[q, 0]),
                pltpu.make_async_copy(ds_last.at[part], b_ds.at[q, CHIPS - 1], loc.at[q, 1])]

    def copies0(q):
        part = pl.ds(q * PIECE + theirs, SHARE)
        logs = pl.ds(q * PIECE, PIECE)
        return [rcopy(sp.at[part], r_s.at[q], send0.at[q, 0], recv0.at[q, 0], partner),
                rcopy(dsp.at[part], r_ds.at[q], send0.at[q, 1], recv0.at[q, 1], partner),
                rcopy(ld.at[logs], r_ld.at[q], send0.at[q, 2], recv0.at[q, 2], partner)]

    def swap(q):
        if q == 0:
            met(chips, planes)
        each(copies0(q) + own_loads(q), "start")

    def copies1(q, c_dst, c_slot):
        part = pl.ds(c_dst * OWN, OWN)
        dev = at_chip(c_dst)
        return [rcopy(c_ld.at[q], p_ld.at[q, c_slot], send1.at[q, 2, c_dst], recv1.at[q, 2, c_slot], dev),
                rcopy(c_s.at[q, part], p_s.at[q, c_slot], send1.at[q, 0, c_dst], recv1.at[q, 0, c_slot], dev),
                rcopy(c_ds.at[q, part], p_ds.at[q, c_slot], send1.at[q, 1, c_dst], recv1.at[q, 1, c_slot], dev)]

    def decay(ref, q, h):
        return jnp.exp2(ref[q, pl.ds(h, 1), :])

    def pairs(q):
        each(copies0(q), "wait")
        c_ld[q] = ld[blk(q, PIECE), :] + r_ld[q]

        @pl.loop(0, SHARE)
        def _(h):
            hh = q * PIECE + mine + h
            own = jnp.exp2(ld[pl.ds(hh, 1), :])
            oth = decay(r_ld, q, mine + h)

            @pl.when(core == 0)
            def _():
                c_s[q, h] = sp[hh] * oth + r_s[q, h]
                c_ds[q, h] = dsp[hh] + own * r_ds[q, h]

            @pl.when(core == 1)
            def _():
                c_s[q, h] = r_s[q, h] * own + sp[hh]
                c_ds[q, h] = r_ds[q, h] + oth * dsp[hh]

        for c in chips:
            each(copies1(q, c, chip), "start")
        p_ld[q, chip] = c_ld[q]

        @pl.loop(0, OWN)
        def _(h):
            p_s[q, chip, h] = c_s[q, chip * OWN + h]
            p_ds[q, chip, h] = c_ds[q, chip * OWN + h]

    def copy2(q, kind, z_dst, z_slot):
        return rcopy((t_s, t_ds)[kind].at[q], z_b.at[q, z_slot], send2.at[q, 0, z_dst], recv2.at[q, 0, z_slot], at_z(z_dst))

    def copy2_ld(q, z_dst, z_slot):
        return rcopy(t_ld.at[q], z_ld.at[q, z_slot], send2.at[q, 1, z_dst], recv2.at[q, 1, z_slot], at_z(z_dst))

    def chip_decays(q, h):
        return [jnp.exp2(p_ld[q, c, pl.ds(mine + chip * OWN + h, 1), :]) for c in ALL_CHIPS]

    def z_decay(q, zz, h):
        return jnp.exp2(z_ld[q, zz, pl.ds(mine + chip * OWN + h, 1), :])

    def plane(q):
        for c in chips:
            each(copies1(q, c, c), "wait_recv")
        t_ld[q] = sum(p_ld[q, c] for c in ALL_CHIPS)

        @pl.loop(0, OWN)
        def _(h):
            d = chip_decays(q, h)
            acc = p_s[q, 0, h]
            for c in ALL_CHIPS[1:]:
                acc = acc * d[c] + p_s[q, c, h]
            t_s[q, h] = acc
            acc = p_ds[q, CHIPS - 1, h]
            for c in ALL_CHIPS[-2::-1]:
                acc = acc * d[c] + p_ds[q, c, h]
            t_ds[q, h] = acc

        for zz in planes:
            copy2_ld(q, zz, z).start()

            @pl.when(zz > z)
            def _():
                copy2(q, 0, zz, z).start()

            @pl.when(zz < z)
            def _():
                copy2(q, 1, zz, z).start()

    def copies3(q, c_dst, c_slot):
        dev = at_chip(c_dst)
        part = pl.ds(c_slot * OWN, OWN)
        return [rcopy(b_s.at[q, c_dst], a_s.at[q, part], send3.at[q, 0, c_dst], recv3.at[q, 0, c_slot], dev),
                rcopy(b_ds.at[q, c_dst], a_ds.at[q, part], send3.at[q, 1, c_dst], recv3.at[q, 1, c_slot], dev)]

    def copy_f(q, zz):
        return rcopy(f_own.at[q], f_all.at[q, pl.ds(chip * OWN, OWN)], send5.at[q, 0, zz], recv5.at[q, 0, chip], at_z(zz))

    def prefix(q):
        for zz in planes:
            copy2_ld(q, zz, zz).wait_recv()
            copy2(q, 0, zz, zz).wait_recv()
        each(own_loads(q), "wait")

        @pl.loop(0, OWN)
        def _(h):
            for zz in range(PLANES - 1):
                @pl.when(zz < z)
                def _():
                    b_s[q, 0, h] = b_s[q, 0, h] * z_decay(q, zz, h) + z_b[q, zz, h]
            for zz in range(PLANES)[:0:-1]:
                @pl.when(zz > z)
                def _():
                    b_ds[q, CHIPS - 1, h] = b_ds[q, CHIPS - 1, h] * z_decay(q, zz, h) + z_b[q, zz, h]
            d = chip_decays(q, h)
            acc = b_s[q, 0, h]
            for c in ALL_CHIPS[:-1]:
                acc = acc * d[c] + p_s[q, c, h]
                b_s[q, c + 1, h] = acc
            acc = b_ds[q, CHIPS - 1, h]
            for c in ALL_CHIPS[:0:-1]:
                acc = acc * d[c] + p_ds[q, c, h]
                b_ds[q, c - 1, h] = acc
            f_own[q, h] = acc * d[0] + p_ds[q, 0, h]
            a_s[q, chip * OWN + h] = b_s[q, chip, h]
            a_ds[q, chip * OWN + h] = b_ds[q, chip, h]

        for c in chips:
            each(copies3(q, c, chip), "start")

    def send_first():
        @pl.when(z == 0)
        def _():
            for q in range(QS):
                for zz in range(1, PLANES):
                    copy_f(q, zz).start()

                @pl.loop(0, OWN)
                def _(h):
                    f_all[q, chip * OWN + h] = f_own[q, h]

    def out_copies(q):
        part = pl.ds(q * PIECE + mine, SHARE)
        return [rcopy(o_s.at[q], start.at[part], send4.at[q, 0], recv4.at[q, 0], partner),
                rcopy(o_ds.at[q], end.at[part], send4.at[q, 1], recv4.at[q, 1], partner),
                pltpu.make_async_copy(n_s.at[q], start.at[part], loc.at[q, 2]),
                pltpu.make_async_copy(n_ds.at[q], end.at[part], loc.at[q, 3])]

    def halve(q):
        for c in chips:
            each(copies3(q, c, c), "wait_recv")

        @pl.loop(0, SHARE)
        def _(h):
            hh = q * PIECE + mine + h
            own = jnp.exp2(ld[pl.ds(hh, 1), :])
            oth = decay(r_ld, q, mine + h)

            @pl.when(core == 0)
            def _():
                n_s[q, h] = a_s[q, h]
                n_ds[q, h] = r_ds[q, h] + oth * a_ds[q, h]
                o_s[q, h] = own * a_s[q, h] + sp[hh]
                o_ds[q, h] = a_ds[q, h]

            @pl.when(core == 1)
            def _():
                n_s[q, h] = oth * a_s[q, h] + r_s[q, h]
                n_ds[q, h] = a_ds[q, h]
                o_s[q, h] = a_s[q, h]
                o_ds[q, h] = dsp[hh] + own * a_ds[q, h]

        each(out_copies(q), "start")

    def copy5(q, c_dst, c_slot):
        part = f_all.at[q, pl.ds(c_slot * OWN, OWN)]
        return rcopy(part, part, send5.at[q, 1, c_dst], recv5.at[q, 1, c_slot], at_chip(c_dst))

    def spread(q):
        @pl.when(z > 0)
        def _():
            copy_f(q, z).wait_recv()

        for c in chips:
            copy5(q, c, chip).start()

    def last(q):
        part = first.at[pl.ds(q * PIECE + mine, SHARE)]
        return [rcopy(f_all.at[q], part, send4.at[q, 2], recv4.at[q, 2], partner),
                pltpu.make_async_copy(f_all.at[q], part, loc.at[q, 4])]

    def sp_copy():
        return [pltpu.make_async_copy(sp, sp_out, loc.at[0, 5])]

    def finish():
        for q in range(QS):
            for c in chips:
                copy5(q, c, c).wait_recv()
            each(last(q), "start")
        for q in range(QS):
            each(out_copies(q), "wait")
            for c in chips:
                each(copies1(q, c, chip) + copies3(q, c, chip) + [copy5(q, c, chip)], "wait_send")
            for zz in planes:
                copy2(q, 0, zz, z).wait_send()
                copy2_ld(q, zz, z).wait_send()

            @pl.when(z == 0)
            def _():
                for zz in range(1, PLANES):
                    copy_f(q, zz).wait_send()
        each(sp_copy(), "wait")
        for q in range(QS):
            each(last(q), "wait")

    early = {0: [hello], 4: [functools.partial(swap, 0)], 6: [functools.partial(pairs, 0)],
             8: [functools.partial(swap, 1), lambda: each(sp_copy(), "start")]}
    late = [(0, 2, functools.partial(pairs, 1)), (1, 2, functools.partial(plane, 0)), (2, 5, functools.partial(plane, 1)),
            (3, 0, functools.partial(prefix, 0)), (4, 3, functools.partial(prefix, 1)), (4, 3, send_first),
            (5, 0, functools.partial(halve, 0)), (6, 2, functools.partial(halve, 1)), (6, 3, functools.partial(spread, 0)),
            (6, 5, functools.partial(spread, 1)), (7, 5, finish)]
    return early, late


def link_shapes():
    st = (HD, N)
    V = pltpu.VMEM
    D = pltpu.SemaphoreType.DMA

    def states(*lead):
        return V((QS,) + lead + st, F32)

    def logs(*lead):
        return V((QS,) + lead + (PIECE, N), F32)

    share, four, own = states(SHARE), states(CHIPS, OWN), states(OWN)
    three = D((QS, 3, CHIPS))
    two = D((QS, 2, CHIPS))
    return [share, share, logs(), share, share, logs(), four, four, logs(CHIPS), own, own, logs(), four, logs(PLANES),
            four, four, share, share, share, share, share, share, own, share,
            D((QS, 3)), D((QS, 3)), three, three, two, two, two, two, D((QS, 3)), D((QS, 3)), two, two, D((QS, 6))]


def local_kernel(nb, ng, x_ref, dy_ref, dt_ref, rate_ref, b_ref, c_ref, s_init, ds_last,
                 du_ref, ry_ref, db_ref, dc_ref, cum_out, start, end, first, sp_out,
                 gram, dgram, s_cur, ds_cur, xw, yw, y_in, u_in, rcol, cums, sp, dsp, ld, *link_scratch):
    step_id = pl.program_id(0)
    early, late = link_steps(ng, sp, dsp, ld, s_init, ds_last, start, end, first, sp_out, *link_scratch)
    for at, steps in early.items():
        @pl.when(step_id == at)
        def _():
            for step in steps:
                step()

    @pl.when(step_id < ng)
    def _():
        range_states(nb, step_id, x_ref, dy_ref, dt_ref, rate_ref, b_ref, c_ref, cum_out, cums, sp, dsp, ld, xw, yw)

    @pl.when(step_id >= ng)
    def _():
        local_group(nb, ng, step_id - ng, late, x_ref, dy_ref, dt_ref, b_ref, c_ref, du_ref, ry_ref, db_ref, dc_ref,
                    gram, dgram, s_cur, ds_cur, xw, yw, y_in, u_in, rcol, cums.at[step_id - ng])


def range_states(nb, g, x_ref, dy_ref, dt_ref, rate_ref, b_ref, c_ref, cum_out, cums, sp, dsp, ld, xw, yw):
    tri = tri_mask(True).astype(BF16)
    dt = dt_ref[...]
    a = dt * rate_ref[:, :1]
    cum, before = [], [jnp.zeros((GH, 1), F32)]
    for i in range(nb):
        v = dot_tri(a[:, blk(i, T)], tri)
        cums[g, :, blk(i, T)] = v
        cum_out[:, blk(i, T)] = v
        cum.append(v)
        before.append(before[-1] + last_col(v))
    ld[pl.ds(pl.multiple_of(g * GH, GH), GH), :] = jnp.broadcast_to(before[nb], (GH, T))
    after = jnp.zeros((GH, 1), F32)
    acc_s = jnp.zeros((GR, N), F32)
    acc_ds = jnp.zeros((GR, N), F32)
    for i in reversed(range(nb)):
        tok = blk(i, T)
        w_in = dt[:, tok] * jnp.exp2((last_col(cum[i]) - cum[i]) + after)
        w_out = jnp.exp2(cum[i] + before[i])
        after = after + last_col(cum[i])
        for j in range(GH):
            rows = blk(j, HD)
            xw[i, rows, :T], xw[i, rows, T:] = split2(x_ref[rows, tok].astype(F32) * row(w_in, j))
            yw[i, rows, :T], yw[i, rows, T:] = split2(dy_ref[rows, tok].astype(F32) * row(w_out, j))
        acc_s += mm(xw[i], cat0(b_ref[tok, :], b_ref[tok, :]))
        acc_ds += mm(yw[i], cat0(c_ref[tok, :], c_ref[tok, :]))
    for j in range(GH):
        sp[g * GH + j] = acc_s[blk(j, HD), :]
        dsp[g * GH + j] = acc_ds[blk(j, HD), :]


def local_group(nb, ng, g, late, x_ref, dy_ref, dt_ref, b_ref, c_ref, du_ref, ry_ref, db_ref, dc_ref,
                gram, dgram, s_cur, ds_cur, xw, yw, y_in, u_in, rcol, cum_ref):
    @pl.when(g == 0)
    def _():
        low = tri_mask(False)
        for i in range(nb):
            tok = blk(i, T)
            gram[i] = mm_nt(c_ref[tok, :], b_ref[tok, :]) * low
            dgram[i] = jnp.zeros((T, T), F32)
        db_ref[...] = jnp.zeros_like(db_ref)
        dc_ref[...] = jnp.zeros_like(dc_ref)
        rcol[...] = jnp.zeros_like(rcol)

    ds_cur[...] = jnp.zeros_like(ds_cur)
    s_cur[...] = jnp.zeros_like(s_cur)

    @pl.loop(0, nb)
    def _(i):
        tok = pl.ds(pl.multiple_of(i * T, T), T)
        cum = cum_ref[:, tok]
        w_in = dt_ref[:, tok] * jnp.exp2(last_col(cum) - cum)
        e_out = jnp.exp2(cum)
        for j in range(GH):
            rows = blk(j, HD)
            hi, lo = split2(x_ref[rows, tok].astype(F32) * row(w_in, j))
            xw[i, rows, :T] = hi
            xw[i, rows, T:] = lo
            hi, lo = split2(dy_ref[rows, tok].astype(F32) * row(e_out, j))
            yw[i, rows, :T] = hi
            yw[i, rows, T:] = lo
            du_ref[rows, tok] = jnp.zeros((HD, T), F32)

    @pl.loop(0, nb)
    def _(i):
        for at_g, at_i, step in late:
            @pl.when((g == at_g) & (i == at_i))
            def _():
                step()

        k = nb - 1 - i
        tok_k = pl.ds(pl.multiple_of(k * T, T), T)
        tok = pl.ds(pl.multiple_of(i * T, T), T)

        cum_k = cum_ref[:, tok_k]
        tot_k = last_col(cum_k)
        ds_hi, ds_lo = split2(ds_cur[...])
        b_k = b_ref[tok_k, :]
        c_k = c_ref[tok_k, :]
        u_in[...] = mm_nt(cat1(ds_hi, ds_lo), cat1(b_k, b_k))
        db2 = mm_tn(xw[k, :, :T], cat1(ds_hi, ds_lo))
        db_ref[tok_k, :] += db2[:, :N] + db2[:, N:] + mm_tn(xw[k, :, T:], ds_hi)
        upd_k = mm(yw[k], cat0(c_k, c_k))
        e_in = jnp.exp2(tot_k - cum_k)
        e_tot_k = jnp.exp2(tot_k)
        for j in range(GH):
            rows = blk(j, HD)
            du_ref[rows, tok_k] += u_in[rows, :] * row(e_in, j)
            ds_cur[rows, :] = ds_cur[rows, :] * row(e_tot_k, j) + upd_k[rows, :]

        cum = cum_ref[:, tok]
        e_tot = jnp.exp2(last_col(cum))
        e_out = jnp.exp2(cum)
        dt = dt_ref[:, tok]
        s_hi, s_lo = split2(s_cur[...])
        b_i = b_ref[tok, :]
        c_i = c_ref[tok, :]
        y_in[...] = mm_nt(cat1(s_hi, s_lo), cat1(c_i, c_i))
        dc2 = mm_tn(yw[i, :, :T], cat1(s_hi, s_lo))
        dc_ref[tok, :] += dc2[:, :N] + dc2[:, N:] + mm_tn(yw[i, :, T:], s_hi)
        upd = mm(xw[i], cat0(b_i, b_i))
        for j in range(GH):
            rows = blk(j, HD)
            s_cur[rows, :] = s_cur[rows, :] * row(e_tot, j) + upd[rows, :]
        cum_c = jnp.transpose(cum)
        g_i = gram[i]
        zero = jnp.zeros((HD, T), BF16)
        inter = []
        for j0 in range(0, GH, 2):
            y_t = jnp.transpose(dy_ref[pl.ds(j0 * HD, T), tok])
            u0, v0 = split2(x_ref[blk(j0, HD), tok].astype(F32) * row(dt, j0))
            u1, v1 = split2(x_ref[blk(j0 + 1, HD), tok].astype(F32) * row(dt, j0 + 1))
            pair = mm(cat1(y_t, y_t), cat1(cat0(u0, zero, v0, zero), cat0(zero, u1, zero, v1)))
            e_sum = None
            for j, p in ((j0, pair[:, :T]), (j0 + 1, pair[:, T:])):
                rows = blk(j, HD)
                lam = jnp.exp2(jnp.minimum(cum_c[:, blk(j, 1)] - row(cum, j), 0.0))
                e_sum = lam * p if e_sum is None else e_sum + lam * p
                m = lam * g_i
                rcol[:, blk(j, 1)] = sum1(m * p)
                m_hi, m_lo = split2(m)
                yb = dy_ref[rows, tok]
                du_ref[rows, tok] += mm(cat1(yb, yb), cat0(m_hi, m_lo))
                inter.append(sum0(yb.astype(F32) * y_in[rows, :]))
            dgram[i] += e_sum
        ry_ref[:, tok] = jnp.transpose(rcol[...])[:GH, :] + e_out * cat0(*inter)

    @pl.when(g == ng - 1)
    def _():
        low_f = tri_mask(False)
        for i in range(nb):
            tok = blk(i, T)
            bb = b_ref[tok, :]
            cc = c_ref[tok, :]
            hi, lo = split2(dgram[i] * low_f)
            dc_ref[tok, :] += mm(hi, bb) + mm(lo, bb)
            db_ref[tok, :] += mm_tn(hi, cc) + mm_tn(lo, cc)


def local_grads(x_t, dy_t, dt_t, rate, b, c, s_init, ds_last):
    rows, seq = x_t.shape
    nb, ng = seq // T, rows // GR
    big = pl.BlockSpec((GR, seq), lambda g: (lax.rem(g, ng), 0))
    head = pl.BlockSpec((GH, seq), lambda g: (lax.rem(g, ng), 0))
    hd1 = pl.BlockSpec((GH, T), lambda g: (lax.rem(g, ng), 0))
    big_o = pl.BlockSpec((GR, seq), lambda g: (jnp.maximum(g - ng, 0), 0))
    head_o = pl.BlockSpec((GH, seq), lambda g: (jnp.maximum(g - ng, 0), 0))
    cum_o = pl.BlockSpec((GH, seq), lambda g: (jnp.minimum(g, ng - 1), 0))
    full = pl.BlockSpec((seq, N), lambda g: (0, 0))
    anyw = pl.BlockSpec(memory_space=pl.ANY)
    sd = jax.ShapeDtypeStruct
    state = sd((HEADS, HD, N), F32)
    V = pltpu.VMEM
    sq, grp, wide = V((nb, T, T), F32), V((GR, N), F32), V((nb, GR, 2 * T), BF16)
    return pl.pallas_call(
        functools.partial(local_kernel, nb, ng),
        grid=(2 * ng,),
        in_specs=[big, big, head, hd1, full, full, anyw, anyw],
        out_specs=[big_o, head_o, full, full, cum_o, anyw, anyw, anyw, anyw],
        out_shape=[sd((rows, seq), F32), sd((rows // HD, seq), F32), sd((seq, N), F32), sd((seq, N), F32),
                   sd((rows // HD, seq), F32), state, state, state, state],
        scratch_shapes=[sq, sq, grp, grp, wide, wide, grp, grp, V((T, T), F32), V((ng, GH, seq), F32),
                        V((HEADS, HD, N), F32), V((HEADS, HD, N), F32), V((HEADS, N), F32)] + link_shapes(),
        compiler_params=pltpu.CompilerParams(dimension_semantics=("arbitrary",), collective_id=0, has_side_effects=True),
        name="local_grads",
    )(x_t, dy_t, dt_t, rate, b, c, s_init, ds_last)


T2 = 256


def join_kernel(nb, ng, x_ref, dy_ref, dt_ref, cum_ref, rate_ref, skip_ref, s0_ref, dse_ref, sp_ref, b_ref, c_ref,
                du_ref, ry_ref, dbl_ref, dcl_ref,
                dx_ref, ddt_ref, dal_ref, dsk_ref, db_ref, dc_ref,
                db_acc, dc_acc, ein, eout, xw, yw, s2, d2, y_in, u_in, dcum, xdu, skt):
    g = pl.program_id(0)

    @pl.when(g == 0)
    def _():
        db_acc[...] = dbl_ref[...]
        dc_acc[...] = dcl_ref[...]

    cums = [cum_ref[:, i * T:(i + 1) * T] for i in range(nb)]
    tots = [last_col(v) for v in cums]
    acc = jnp.zeros_like(tots[0])
    for i in range(nb):
        eout[:, i * T:(i + 1) * T] = jnp.exp2(cums[i] + acc)
        acc = acc + tots[i]
    e_tot = jnp.exp2(acc)
    acc = jnp.zeros_like(tots[0])
    for i in reversed(range(nb)):
        ein[:, i * T:(i + 1) * T] = jnp.exp2((tots[i] - cums[i]) + acc)
        acc = acc + tots[i]

    s_hi, s_lo = split2(s0_ref[...])
    d_hi, d_lo = split2(dse_ref[...])
    s2[...] = cat1(s_hi, s_lo)
    d2[...] = cat1(d_hi, d_lo)

    @pl.loop(0, nb * T // T2)
    def _(i):
        tok = pl.ds(pl.multiple_of(i * T2, T2), T2)
        bb = b_ref[tok, :]
        cc = c_ref[tok, :]
        y_in[...] = mm_nt(s2[...], cat1(cc, cc))
        u_in[...] = mm_nt(d2[...], cat1(bb, bb))
        dt = dt_ref[:, tok]
        e_in = ein[:, tok]
        e_out = eout[:, tok]
        w_in = dt * e_in
        xds, rys, sks = [], [], []
        for j in range(GH):
            rows = blk(j, HD)
            xf = x_ref[rows, tok].astype(F32)
            yf = dy_ref[rows, tok].astype(F32)
            du = du_ref[rows, tok] + row(e_in, j) * u_in[rows, :]
            dx_ref[rows, tok] = (row(dt, j) * du + skip_ref[blk(j, 1), :1] * yf).astype(BF16)
            xds.append(sum0(xf * du))
            rys.append(sum0(yf * y_in[rows, :]))
            sks.append(sum0(xf * yf))
            xw[rows, :T2], xw[rows, T2:] = split2(xf * row(w_in, j))
            yw[rows, :T2], yw[rows, T2:] = split2(yf * row(e_out, j))
        dc2 = mm_tn(yw[:, :T2], s2[...])
        dc_acc[tok, :] += dc2[:, :N] + dc2[:, N:] + mm_tn(yw[:, T2:], s2[:, :N])
        db2 = mm_tn(xw[:, :T2], d2[...])
        db_acc[tok, :] += db2[:, :N] + db2[:, N:] + mm_tn(xw[:, T2:], d2[:, :N])
        xd = cat0(*xds)
        xdu[:, tok] = xd
        dcum[:, tok] = ry_ref[:, tok] + e_out * cat0(*rys) - dt * xd
        skt[:, tok] = cat0(*sks)

    for j in range(GH):
        rows = blk(j, HD)
        dal_ref[j:j + 1, :] = jnp.sum(dse_ref[rows, :] * (sp_ref[rows, :] + row(e_tot, j) * s0_ref[rows, :]), axis=0, keepdims=True)
    run = jnp.sum(dal_ref[...], axis=1, keepdims=True)
    rate = rate_ref[...] * (1.0 / LOG2E)
    low = tri_mask(False).astype(BF16)
    total = jnp.zeros((GH, T), F32)
    for i in reversed(range(nb)):
        tok = blk(i, T)
        da = dot_tri(dcum[:, tok], low) + run
        run = da[:, 0:1]
        da = da * rate
        ddt_ref[:, tok] = xdu[:, tok] + da
        total = total + dt_ref[:, tok] * da
    dal_ref[...] = jnp.broadcast_to(jnp.sum(total, axis=1, keepdims=True), (GH, T))
    dsk_ref[...] = jnp.broadcast_to(jnp.sum(skt[...], axis=1, keepdims=True), (GH, T))

    @pl.when(g == ng - 1)
    def _():
        db_ref[...] = db_acc[...].astype(BF16)
        dc_ref[...] = dc_acc[...].astype(BF16)


def join_grads(x_t, dy_t, dt_t, cum, rate, skip, s0, dse, sp, b, c, du, ry, dbl, dcl):
    rows, seq = x_t.shape
    nb, ng = seq // T, rows // GR
    big = pl.BlockSpec((GR, seq), lambda g: (g, 0))
    head = pl.BlockSpec((GH, seq), lambda g: (g, 0))
    hd1 = pl.BlockSpec((GH, T), lambda g: (g, 0))
    full = pl.BlockSpec((seq, N), lambda g: (0, 0))
    st = pl.BlockSpec((GR, N), lambda g: (g, 0))
    sd = jax.ShapeDtypeStruct
    return pl.pallas_call(
        functools.partial(join_kernel, nb, ng),
        grid=(ng,),
        in_specs=[big, big, head, head, hd1, hd1, st, st, st, full, full, big, head, full, full],
        out_specs=[big, head, hd1, hd1, full, full],
        out_shape=[sd((rows, seq), BF16), sd((rows // HD, seq), F32), sd((rows // HD, T), F32),
                   sd((rows // HD, T), F32), sd((seq, N), BF16), sd((seq, N), BF16)],
        scratch_shapes=[pltpu.VMEM((seq, N), F32), pltpu.VMEM((seq, N), F32),
                        pltpu.VMEM((GH, seq), F32), pltpu.VMEM((GH, seq), F32),
                        pltpu.VMEM((GR, 2 * T2), BF16), pltpu.VMEM((GR, 2 * T2), BF16),
                        pltpu.VMEM((GR, 2 * N), BF16), pltpu.VMEM((GR, 2 * N), BF16),
                        pltpu.VMEM((GR, T2), F32), pltpu.VMEM((GR, T2), F32),
                        pltpu.VMEM((GH, seq), F32), pltpu.VMEM((GH, seq), F32), pltpu.VMEM((GH, seq), F32)],
        compiler_params=pltpu.CompilerParams(dimension_semantics=("arbitrary",)),
        name="join_grads",
    )(x_t, dy_t, dt_t, cum, rate, skip, s0, dse, sp, b, c, du, ry, dbl, dcl)

def sum_kernel(dal_ref, dsk_ref, out_ref, v1, v2, v3, send, recv):
    core, chip, z, partner, chips, planes, at_chip, at_z = neighbours()
    greet(partner, chips, planes, at_chip, at_z)
    v1[core] = cat0(jnp.transpose(dal_ref[...])[:OWN, :], jnp.transpose(dsk_ref[...])[:OWN, :])
    met(chips, planes)

    def copy(buf, stage, to, slot, dev):
        return rcopy(buf.at[slot], buf.at[slot], send.at[stage, to], recv.at[stage, slot], dev)

    def exchange(buf, stage, me, others, at):
        each([copy(buf, stage, o, me, at(o)) for o in others], "start")
        each([copy(buf, stage, o, o, at(o)) for o in others], "wait_recv")
        each([copy(buf, stage, o, me, at(o)) for o in others], "wait_send")

    exchange(v1, 0, core, [1 - core], lambda o: partner)
    v2[chip] = v1[0] + v1[1]
    exchange(v2, 1, chip, chips, at_chip)
    v3[z] = sum(v2[c] for c in ALL_CHIPS)
    exchange(v3, 2, z, planes, at_z)
    out_ref[...] = sum(v3[p] for p in range(PLANES))


def sum_devices(dal, dsk):
    vm = pl.BlockSpec(memory_space=pltpu.VMEM)
    V = pltpu.VMEM
    out = pl.pallas_call(
        sum_kernel,
        in_specs=[vm, vm],
        out_specs=vm,
        out_shape=jax.ShapeDtypeStruct((2 * OWN, HEADS), F32),
        scratch_shapes=[V((2, 2 * OWN, HEADS), F32), V((CHIPS, 2 * OWN, HEADS), F32), V((PLANES, 2 * OWN, HEADS), F32),
                        pltpu.SemaphoreType.DMA((3, CHIPS)), pltpu.SemaphoreType.DMA((3, CHIPS))],
        compiler_params=pltpu.CompilerParams(collective_id=1, has_side_effects=True),
        name="sum_devices",
    )(dal, dsk)
    return out[0], out[OWN]


def solution(mesh):
    tok4 = P(None, AXIS, None, None)
    tok3 = P(None, AXIS, None)

    def device_step(x_loc, dt_loc, a_log, b_loc, c_loc, d_skip, s_init, dy_loc, ds_last):
        seq = x_loc.shape[1]
        x_t = x_loc[0].transpose(1, 2, 0).reshape(HEADS * HD, seq)
        dy_t = dy_loc[0].transpose(1, 2, 0).reshape(HEADS * HD, seq)
        dt_t = dt_loc[0].T
        rate = jnp.broadcast_to((-jnp.exp(a_log) * LOG2E)[:, None], (HEADS, T))
        skip = jnp.broadcast_to(d_skip[:, None], (HEADS, T))
        b, c = b_loc[0], c_loc[0]
        flat = (HEADS * HD, N)
        du, ry, dbl, dcl, cum, start, end, first, sp = local_grads(x_t, dy_t, dt_t, rate, b, c, s_init[0], ds_last[0])
        dx, ddt, dal, dsk, db, dc = join_grads(x_t, dy_t, dt_t, cum, rate, skip, start.reshape(flat), end.reshape(flat),
                                               sp.reshape(flat), b, c, du, ry, dbl, dcl)
        grad_x = dx.reshape(HEADS, HD, seq).transpose(2, 0, 1)[None]
        grad_alog, grad_skip = sum_devices(dal, dsk)
        return grad_x, ddt.T[None], db[None], dc[None], first[None], grad_alog, grad_skip

    return jax.shard_map(device_step, mesh=mesh,
                         in_specs=(tok4, tok3, P(), tok3, tok3, P(), P(), tok4, P()),
                         out_specs=(tok4, tok3, tok3, tok3, P(), P(), P()),
                         check_vma=False)
```

time: 1290 us -> 142 us (0.11)
  matrix products: 519 us -> 0 us
  waiting for transfers between devices: 452 us -> 0 us
  local copies, waits for them, and re-layouts: 153 us -> 4.61 us
  Pallas kernels: 0 us -> 135 us
  blocking collectives: 82.2 us -> 0 us
  other arithmetic: 39.3 us -> 0.66 us
  loops' own time: 25.1 us -> 0 us
  between operations: 14.6 us -> 0.67 us
    dot_general x38 -> x0, matrix products: 519 us -> none  [the longest x6 141 us: chunk_step(): jnp.einsum('btsh,bshp->bthp', mix_mat, u_blk, precision=HIGH_PREC, prefer...]
    all_gather x2 -> x0, waiting for transfers between devices: 452 us -> none  [the longest x1 265 us: device_step(): grad_all = lax.all_gather(grad_part, AXIS)]
    pallas_call x0 -> x3, Pallas kernels: none -> 135 us  [the longest x1 87.8 us: local_grads(): pl.pallas_call(functools.partial(local_kernel, nb, ng), grid=(2 * ng,), i...]
    squeeze x15 -> x1, local copies, waits for them, and re-layouts: 72.9 us -> 1.26 us  [sum_devices(): return (out[0], out[OWN])]
    all_gather x1 -> x0, blocking collectives: 43.8 us -> none  [device_step(): logdec_all = lax.all_gather(log_part, AXIS)]
    psum x1 -> x0, blocking collectives: 38.5 us -> none  [device_step(): grad_alog, grad_skip = lax.psum((grad_alog, grad_skip), AXIS)]
    another operation x2 -> x0, loops' own time: 25.1 us -> none  [span_step(): return lax.scan(inner_step, carry_state, span_in)]
    dynamic_slice x3 -> x0, local copies, waits for them, and re-layouts: 22.1 us -> none  [span_step(): return lax.scan(inner_step, carry_state, span_in)]
  transfers between devices with their start and end apart: 2 -> 0, of which waited for: 2 -> 0; matrix products, arithmetic and copies ran while one was open for 17% -> 0% of each run, Pallas kernels for 0% -> 0%
where the time goes in v2:
time: 142 us; the launch traced here: 141 us
  Pallas kernels  135 us (95%)
  local copies, waits for them, and re-layouts  4.61 us (3%)
    pallas_call x1, Pallas kernels, local_grads(): pl.pallas_call(functools.partial(local_kernel, nb, ng), grid=(2 * ng,), i...  87.8 us
    pallas_call x1, Pallas kernels, join_grads(): pl.pallas_call(functools.partial(join_kernel, nb, ng), grid=(ng,), in_spe...  30.6 us
    pallas_call x1, Pallas kernels, sum_devices(): pl.pallas_call(sum_kernel, in_specs=[vm, vm], out_specs=vm, out_shape=jax...  16.9 us

profile of v2, /device:TPU:0, one launch (start us, length us, event | category | flops | bytes accessed | tf_op | source)
XLA Modules:
  0.0 141.3 jit_solution(4806360329194401780)
XLA Ops:
  0.6 0.7 negate_multiply_fusion
  1.3 0.7 broadcast_in_dim.27.rate_ref
  2.0 1.3 broadcast_in_dim.28.skip_ref
  3.3 87.8 %local_grads.1 = (f32[4096,768]{1,0:T(8,128)}, f32[64,768]{1,0:T(8,128)}, f32[768,128]{1,0:T(8,128)}, f32[768,128]{1,0:T(8,128)}, f32[64,768]{1,0:T(8,128)}, /*i...) custom-call(bf16[4096,768]{1,0:T(8,128)(2,1)} %bitcast.35, ...), custom_call_target="tpu_custom_call" | custom-call | tf_op jit(solution)/shard_map/local_grads/pallas_call | solution.py:558
  91.1 0.0 copy-start
  91.1 30.6 %join_grads.1 = (bf16[4096,768]{1,0:T(8,128)(2,1)}, f32[64,768]{1,0:T(8,128)}, f32[64,128]{1,0:T(8,128)}, f32[64,128]{1,0:T(8,128)}, bf16[768,128]{1,0:T(8,128)(2,1)}, /*index=5*/bf16[768,128]{1,0:T(8,128)(2,1)}) custom-call(bf16[4096,768]{1,0:T(8,128)(2,1)} %bitcast.36, bf16[4096,768]{1,0:T(8,128)(2,1)} %bitcast.38, f32[64,768]{1,0:T(8,128)} %bitcast.46, ...), custom_call_target="tpu_custom_call" | custom-call | tf_op jit(solution)/shard_map/join_grads/pallas_call | solution.py:667
  121.7 16.9 %sum_devices.1 = f32[8,64]{1,0:T(8,128)} custom-call(f32[64,128]{1,0:T(8,128)} %get-tuple-element.35.dal_ref, f32[64,128]{1,0:T(8,128)} %get-tuple-element.36.dsk_ref), custom_call_target="tpu_custom_call" | custom-call | tf_op jit(solution)/shard_map/sum_devices/pallas_call | solution.py:709
  138.7 1.3 slice_bitcast_fusion
  139.9 0.0 copy-done
  139.9 1.3 copy.17
Async XLA Ops:
  91.1 48.8 %copy-start = (f32[64,64,128]{2,1,0:T(8,128)S(1)}, f32[64,64,128]{2,1,0:T(8,128)}, u32[]{:S(2)}) copy-start(f32[64,64,128]{2,1,0:T(8,128)} %get-tuple-element.34) | copy-start | bytes 6291460

commit v3 on v2

--- a/solution.py
+++ b/solution.py
@@ -73,6 +73,14 @@
 def dot_tri(v, tri):
     hi, mid, lo = split3(v)
     return mm(hi, tri) + mm(mid, tri) + mm(lo, tri)
+
+
+def columns(ref, v):
+    ref[...] = jnp.transpose(jnp.broadcast_to(v, (T, HEADS)))
+
+
+def group(ref, g):
+    return ref[pl.ds(pl.multiple_of(g * GH, GH), GH), :]
 
 
 def tri_mask(upper):
@@ -380,9 +388,9 @@
             D((QS, 3)), D((QS, 3)), three, three, two, two, two, two, D((QS, 3)), D((QS, 3)), two, two, D((QS, 6))]
 
 
-def local_kernel(nb, ng, x_ref, dy_ref, dt_ref, rate_ref, b_ref, c_ref, s_init, ds_last,
+def local_kernel(nb, ng, x_ref, dy_ref, dt_ref, alog_ref, b_ref, c_ref, s_init, ds_last,
                  du_ref, ry_ref, db_ref, dc_ref, cum_out, start, end, first, sp_out,
-                 gram, dgram, s_cur, ds_cur, xw, yw, y_in, u_in, rcol, cums, sp, dsp, ld, *link_scratch):
+                 gram, dgram, s_cur, ds_cur, xw, yw, y_in, u_in, rcol, cums, rates, sp, dsp, ld, *link_scratch):
     step_id = pl.program_id(0)
     early, late = link_steps(ng, sp, dsp, ld, s_init, ds_last, start, end, first, sp_out, *link_scratch)
     for at, steps in early.items():
@@ -391,9 +399,13 @@
             for step in steps:
                 step()
 
+    @pl.when(step_id == 0)
+    def _():
+        columns(rates, -jnp.exp(alog_ref[...]) * LOG2E)
+
     @pl.when(step_id < ng)
     def _():
-        range_states(nb, step_id, x_ref, dy_ref, dt_ref, rate_ref, b_ref, c_ref, cum_out, cums, sp, dsp, ld, xw, yw)
+        range_states(nb, step_id, x_ref, dy_ref, dt_ref, group(rates, step_id), b_ref, c_ref, cum_out, cums, sp, dsp, ld, xw, yw)
 
     @pl.when(step_id >= ng)
     def _():
@@ -401,10 +413,10 @@
                     gram, dgram, s_cur, ds_cur, xw, yw, y_in, u_in, rcol, cums.at[step_id - ng])
 
 
-def range_states(nb, g, x_ref, dy_ref, dt_ref, rate_ref, b_ref, c_ref, cum_out, cums, sp, dsp, ld, xw, yw):
+def range_states(nb, g, x_ref, dy_ref, dt_ref, rate, b_ref, c_ref, cum_out, cums, sp, dsp, ld, xw, yw):
     tri = tri_mask(True).astype(BF16)
     dt = dt_ref[...]
-    a = dt * rate_ref[:, :1]
+    a = dt * rate[:, :1]
     cum, before = [], [jnp.zeros((GH, 1), F32)]
     for i in range(nb):
         v = dot_tri(a[:, blk(i, T)], tri)
@@ -540,12 +552,12 @@
             db_ref[tok, :] += mm_tn(hi, cc) + mm_tn(lo, cc)
 
 
-def local_grads(x_t, dy_t, dt_t, rate, b, c, s_init, ds_last):
+def local_grads(x_t, dy_t, dt_t, a_log, b, c, s_init, ds_last):
     rows, seq = x_t.shape
     nb, ng = seq // T, rows // GR
     big = pl.BlockSpec((GR, seq), lambda g: (lax.rem(g, ng), 0))
     head = pl.BlockSpec((GH, seq), lambda g: (lax.rem(g, ng), 0))
-    hd1 = pl.BlockSpec((GH, T), lambda g: (lax.rem(g, ng), 0))
+    per_head = pl.BlockSpec((1, HEADS), lambda g: (0, 0))
     big_o = pl.BlockSpec((GR, seq), lambda g: (jnp.maximum(g - ng, 0), 0))
     head_o = pl.BlockSpec((GH, seq), lambda g: (jnp.maximum(g - ng, 0), 0))
     cum_o = pl.BlockSpec((GH, seq), lambda g: (jnp.minimum(g, ng - 1), 0))
@@ -558,31 +570,37 @@
     return pl.pallas_call(
         functools.partial(local_kernel, nb, ng),
         grid=(2 * ng,),
-        in_specs=[big, big, head, hd1, full, full, anyw, anyw],
+        in_specs=[big, big, head, per_head, full, full, anyw, anyw],
         out_specs=[big_o, head_o, full, full, cum_o, anyw, anyw, anyw, anyw],
         out_shape=[sd((rows, seq), F32), sd((rows // HD, seq), F32), sd((seq, N), F32), sd((seq, N), F32),
                    sd((rows // HD, seq), F32), state, state, state, state],
         scratch_shapes=[sq, sq, grp, grp, wide, wide, grp, grp, V((T, T), F32), V((ng, GH, seq), F32),
+                        V((HEADS, T), F32),
                         V((HEADS, HD, N), F32), V((HEADS, HD, N), F32), V((HEADS, N), F32)] + link_shapes(),
         compiler_params=pltpu.CompilerParams(dimension_semantics=("arbitrary",), collective_id=0, has_side_effects=True),
         name="local_grads",
-    )(x_t, dy_t, dt_t, rate, b, c, s_init, ds_last)
+    )(x_t, dy_t, dt_t, a_log, b, c, s_init, ds_last)
 
 
 T2 = 256
 
 
-def join_kernel(nb, ng, x_ref, dy_ref, dt_ref, cum_ref, rate_ref, skip_ref, s0_ref, dse_ref, sp_ref, b_ref, c_ref,
-                du_ref, ry_ref, dbl_ref, dcl_ref,
-                dx_ref, ddt_ref, dal_ref, dsk_ref, db_ref, dc_ref,
-                db_acc, dc_acc, ein, eout, xw, yw, s2, d2, y_in, u_in, dcum, xdu, skt):
+def join_kernel(nb, ng, x_ref, dy_ref, dt_ref, cum_ref, alog_ref, dskip_ref, s0_ref, dse_ref, sp_ref, b_ref, c_ref,
+                du_ref, ry_ref, dbl_ref, dcl_ref, f_ref,
+                dx_ref, ddt_ref, dal_ref, dsk_ref, db_ref, dc_ref, first_ref,
+                rates, skips, db_acc, dc_acc, ein, eout, xw, yw, s2, d2, y_in, u_in, dcum, xdu, skt):
     g = pl.program_id(0)
 
     @pl.when(g == 0)
     def _():
         db_acc[...] = dbl_ref[...]
         dc_acc[...] = dcl_ref[...]
-
+        columns(rates, -jnp.exp(alog_ref[...]))
+        columns(skips, dskip_ref[...])
+
+    first_ref[...] = f_ref[...]
+    rate = group(rates, g)
+    skip = group(skips, g)[:, :1]
     cums = [cum_ref[:, i * T:(i + 1) * T] for i in range(nb)]
     tots = [last_col(v) for v in cums]
     acc = jnp.zeros_like(tots[0])
@@ -600,9 +618,8 @@
     s2[...] = cat1(s_hi, s_lo)
     d2[...] = cat1(d_hi, d_lo)
 
-    @pl.loop(0, nb * T // T2)
-    def _(i):
-        tok = pl.ds(pl.multiple_of(i * T2, T2), T2)
+    for i in range(nb * T // T2):
+        tok = blk(i, T2)
         bb = b_ref[tok, :]
         cc = c_ref[tok, :]
         y_in[...] = mm_nt(s2[...], cat1(cc, cc))
@@ -617,7 +634,7 @@
             xf = x_ref[rows, tok].astype(F32)
             yf = dy_ref[rows, tok].astype(F32)
             du = du_ref[rows, tok] + row(e_in, j) * u_in[rows, :]
-            dx_ref[rows, tok] = (row(dt, j) * du + skip_ref[blk(j, 1), :1] * yf).astype(BF16)
+            dx_ref[rows, tok] = (row(dt, j) * du + row(skip, j) * yf).astype(BF16)
             xds.append(sum0(xf * du))
             rys.append(sum0(yf * y_in[rows, :]))
             sks.append(sum0(xf * yf))
@@ -636,7 +653,6 @@
         rows = blk(j, HD)
         dal_ref[j:j + 1, :] = jnp.sum(dse_ref[rows, :] * (sp_ref[rows, :] + row(e_tot, j) * s0_ref[rows, :]), axis=0, keepdims=True)
     run = jnp.sum(dal_ref[...], axis=1, keepdims=True)
-    rate = rate_ref[...] * (1.0 / LOG2E)
     low = tri_mask(False).astype(BF16)
     total = jnp.zeros((GH, T), F32)
     for i in reversed(range(nb)):
@@ -655,23 +671,25 @@
         dc_ref[...] = dc_acc[...].astype(BF16)
 
 
-def join_grads(x_t, dy_t, dt_t, cum, rate, skip, s0, dse, sp, b, c, du, ry, dbl, dcl):
+def join_grads(x_t, dy_t, dt_t, cum, a_log, d_skip, s0, dse, sp, b, c, du, ry, dbl, dcl, first):
     rows, seq = x_t.shape
     nb, ng = seq // T, rows // GR
     big = pl.BlockSpec((GR, seq), lambda g: (g, 0))
     head = pl.BlockSpec((GH, seq), lambda g: (g, 0))
     hd1 = pl.BlockSpec((GH, T), lambda g: (g, 0))
+    per_head = pl.BlockSpec((1, HEADS), lambda g: (0, 0))
     full = pl.BlockSpec((seq, N), lambda g: (0, 0))
     st = pl.BlockSpec((GR, N), lambda g: (g, 0))
     sd = jax.ShapeDtypeStruct
     return pl.pallas_call(
         functools.partial(join_kernel, nb, ng),
         grid=(ng,),
-        in_specs=[big, big, head, head, hd1, hd1, st, st, st, full, full, big, head, full, full],
-        out_specs=[big, head, hd1, hd1, full, full],
+        in_specs=[big, big, head, head, per_head, per_head, st, st, st, full, full, big, head, full, full, st],
+        out_specs=[big, head, hd1, hd1, full, full, st],
         out_shape=[sd((rows, seq), BF16), sd((rows // HD, seq), F32), sd((rows // HD, T), F32),
-                   sd((rows // HD, T), F32), sd((seq, N), BF16), sd((seq, N), BF16)],
-        scratch_shapes=[pltpu.VMEM((seq, N), F32), pltpu.VMEM((seq, N), F32),
+                   sd((rows // HD, T), F32), sd((seq, N), BF16), sd((seq, N), BF16), sd((rows, N), F32)],
+        scratch_shapes=[pltpu.VMEM((HEADS, T), F32), pltpu.VMEM((HEADS, T), F32),
+                        pltpu.VMEM((seq, N), F32), pltpu.VMEM((seq, N), F32),
                         pltpu.VMEM((GH, seq), F32), pltpu.VMEM((GH, seq), F32),
                         pltpu.VMEM((GR, 2 * T2), BF16), pltpu.VMEM((GR, 2 * T2), BF16),
                         pltpu.VMEM((GR, 2 * N), BF16), pltpu.VMEM((GR, 2 * N), BF16),
@@ -679,9 +697,9 @@
                         pltpu.VMEM((GH, seq), F32), pltpu.VMEM((GH, seq), F32), pltpu.VMEM((GH, seq), F32)],
         compiler_params=pltpu.CompilerParams(dimension_semantics=("arbitrary",)),
         name="join_grads",
-    )(x_t, dy_t, dt_t, cum, rate, skip, s0, dse, sp, b, c, du, ry, dbl, dcl)
-
-def sum_kernel(dal_ref, dsk_ref, out_ref, v1, v2, v3, send, recv):
+    )(x_t, dy_t, dt_t, cum, a_log, d_skip, s0, dse, sp, b, c, du, ry, dbl, dcl, first)
+
+def sum_kernel(dal_ref, dsk_ref, al_ref, sk_ref, v1, v2, v3, send, recv):
     core, chip, z, partner, chips, planes, at_chip, at_z = neighbours()
     greet(partner, chips, planes, at_chip, at_z)
     v1[core] = cat0(jnp.transpose(dal_ref[...])[:OWN, :], jnp.transpose(dsk_ref[...])[:OWN, :])
@@ -700,23 +718,25 @@
     exchange(v2, 1, chip, chips, at_chip)
     v3[z] = sum(v2[c] for c in ALL_CHIPS)
     exchange(v3, 2, z, planes, at_z)
-    out_ref[...] = sum(v3[p] for p in range(PLANES))
+    total = sum(v3[p] for p in range(PLANES))
+    al_ref[...] = row(total, 0)
+    sk_ref[...] = row(total, OWN)
 
 
 def sum_devices(dal, dsk):
     vm = pl.BlockSpec(memory_space=pltpu.VMEM)
     V = pltpu.VMEM
-    out = pl.pallas_call(
+    al, sk = pl.pallas_call(
         sum_kernel,
         in_specs=[vm, vm],
-        out_specs=vm,
-        out_shape=jax.ShapeDtypeStruct((2 * OWN, HEADS), F32),
+        out_specs=[vm, vm],
+        out_shape=[jax.ShapeDtypeStruct((1, HEADS), F32)] * 2,
         scratch_shapes=[V((2, 2 * OWN, HEADS), F32), V((CHIPS, 2 * OWN, HEADS), F32), V((PLANES, 2 * OWN, HEADS), F32),
                         pltpu.SemaphoreType.DMA((3, CHIPS)), pltpu.SemaphoreType.DMA((3, CHIPS))],
         compiler_params=pltpu.CompilerParams(collective_id=1, has_side_effects=True),
         name="sum_devices",
     )(dal, dsk)
-    return out[0], out[OWN]
+    return al[0], sk[0]
 
 
 def solution(mesh):
@@ -728,16 +748,16 @@
         x_t = x_loc[0].transpose(1, 2, 0).reshape(HEADS * HD, seq)
         dy_t = dy_loc[0].transpose(1, 2, 0).reshape(HEADS * HD, seq)
         dt_t = dt_loc[0].T
-        rate = jnp.broadcast_to((-jnp.exp(a_log) * LOG2E)[:, None], (HEADS, T))
-        skip = jnp.broadcast_to(d_skip[:, None], (HEADS, T))
+        a_row, d_row = a_log[None], d_skip[None]
         b, c = b_loc[0], c_loc[0]
         flat = (HEADS * HD, N)
-        du, ry, dbl, dcl, cum, start, end, first, sp = local_grads(x_t, dy_t, dt_t, rate, b, c, s_init[0], ds_last[0])
-        dx, ddt, dal, dsk, db, dc = join_grads(x_t, dy_t, dt_t, cum, rate, skip, start.reshape(flat), end.reshape(flat),
-                                               sp.reshape(flat), b, c, du, ry, dbl, dcl)
+        du, ry, dbl, dcl, cum, start, end, first, sp = local_grads(x_t, dy_t, dt_t, a_row, b, c, s_init[0], ds_last[0])
+        dx, ddt, dal, dsk, db, dc, ds_first = join_grads(x_t, dy_t, dt_t, cum, a_row, d_row, start.reshape(flat),
+                                                         end.reshape(flat), sp.reshape(flat), b, c, du, ry, dbl, dcl,
+                                                         first.reshape(flat))
         grad_x = dx.reshape(HEADS, HD, seq).transpose(2, 0, 1)[None]
         grad_alog, grad_skip = sum_devices(dal, dsk)
-        return grad_x, ddt.T[None], db[None], dc[None], first[None], grad_alog, grad_skip
+        return grad_x, ddt.T[None], db[None], dc[None], ds_first.reshape(HEADS, HD, N)[None], grad_alog, grad_skip
 
     return jax.shard_map(device_step, mesh=mesh,
                          in_specs=(tok4, tok3, P(), tok3, tok3, P(), P(), tok4, P()),

time: 142 us -> 133 us (0.937)
  Pallas kernels: 135 us -> 130 us
  local copies, waits for them, and re-layouts: 4.61 us -> 2.32 us
    pallas_call x1, Pallas kernels: 30.6 us -> 24.6 us  [join_grads(): pl.pallas_call(functools.partial(join_kernel, nb, ng), grid=(ng,), in_spe...]
    broadcast_in_dim x2 -> x0, local copies, waits for them, and re-layouts: 2.02 us -> none  [the longest x1 1.33 us: device_step(): skip = jnp.broadcast_to(d_skip[:, None], (HEADS, T))]
where the time goes in v3:
time: 133 us
  Pallas kernels  130 us (98%)
  local copies, waits for them, and re-layouts  2.32 us (2%)
    pallas_call x1, Pallas kernels, local_grads(): pl.pallas_call(functools.partial(local_kernel, nb, ng), grid=(2 * ng,), i...  88.1 us
    pallas_call x1, Pallas kernels, join_grads(): pl.pallas_call(functools.partial(join_kernel, nb, ng), grid=(ng,), in_spe...  24.6 us
    pallas_call x1, Pallas kernels, sum_devices(): pl.pallas_call(sum_kernel, in_specs=[vm, vm], out_specs=[vm, vm], out_sha...  16.9 us

profile of v3, /device:TPU:0, one launch (start us, length us, event | category | flops | bytes accessed | tf_op | source)
XLA Modules:
  0.0 132.6 jit_solution(8012233472420739167)
XLA Ops:
  0.6 88.1 %local_grads.1 = (f32[4096,768]{1,0:T(8,128)}, f32[64,768]{1,0:T(8,128)}, f32[768,128]{1,0:T(8,128)}, f32[768,128]{1,0:T(8,128)}, f32[64,768]{1,0:T(8,128)}, /*i...) custom-call(bf16[4096,768]{1,0:T(8,128)(2,1)} %bitcast.36, ...), custom_call_target="tpu_custom_call" | custom-call | tf_op jit(solution)/shard_map/local_grads/pallas_call | solution.py:570
  88.8 24.6 %join_grads.1 = (bf16[4096,768]{1,0:T(8,128)(2,1)}, f32[64,768]{1,0:T(8,128)}, f32[64,128]{1,0:T(8,128)}, f32[64,128]{1,0:T(8,128)}, bf16[768,128]{1,0:T(8,128)(...) custom-call(bf16[4096,768]{1,0:T(8,128)(2,1)} %bitcast.37, bf16[4096,768]{1,0:T(8,128)(2,1)} %bitcast.39, ...), custom_call_target="tpu_custom_call" | custom-call | tf_op jit(solution)/shard_map/join_grads/pallas_call | solution.py:684
  113.4 16.9 %sum_devices.1 = (f32[1,64]{1,0:T(1,128)}, f32[1,64]{1,0:T(1,128)}) custom-call(f32[64,128]{1,0:T(8,128)} %get-tuple-element.39.dal_ref, f32[64,128]{1,0:T(8,128)} %get-tuple-element.40.dsk_ref), custom_call_target="tpu_custom_call" | custom-call | tf_op jit(solution)/shard_map/sum_devices/pallas_call | solution.py:729
  130.3 1.2 copy.18
  131.5 1.1 copy.19

commit v4 on v3

--- a/solution.py
+++ b/solution.py
@@ -130,7 +130,7 @@
 
 def link_steps(ng, sp, dsp, ld, s_init, ds_last, start, end, first, sp_out,
                r_s, r_ds, r_ld, c_s, c_ds, c_ld, p_s, p_ds, p_ld, t_s, t_ds, t_ld, z_b, z_ld,
-               b_s, b_ds, a_s, a_ds, n_s, n_ds, o_s, o_ds, f_own, f_all,
+               b_s, b_ds, a_s, a_ds, n_s, n_ds, f_own, f_all,
                send0, recv0, send1, recv1, send2, recv2, send3, recv3, send4, recv4, send5, recv5, loc):
     core, chip, z, partner, chips, planes, at_chip, at_z = neighbours()
     mine, theirs = core * SHARE, (1 - core) * SHARE
@@ -165,32 +165,32 @@
     def decay(ref, q, h):
         return jnp.exp2(ref[q, pl.ds(h, 1), :])
 
+    def by_core(q, lower, upper):
+        for k, run in enumerate((lower, upper)):
+            @pl.when(core == k)
+            def _():
+                for h in range(SHARE):
+                    hh = q * PIECE + mine + h
+                    run(h, hh, jnp.exp2(ld[pl.ds(hh, 1), :]), decay(r_ld, q, mine + h))
+
     def pairs(q):
         each(copies0(q), "wait")
         c_ld[q] = ld[blk(q, PIECE), :] + r_ld[q]
 
-        @pl.loop(0, SHARE)
-        def _(h):
-            hh = q * PIECE + mine + h
-            own = jnp.exp2(ld[pl.ds(hh, 1), :])
-            oth = decay(r_ld, q, mine + h)
-
-            @pl.when(core == 0)
-            def _():
-                c_s[q, h] = sp[hh] * oth + r_s[q, h]
-                c_ds[q, h] = dsp[hh] + own * r_ds[q, h]
-
-            @pl.when(core == 1)
-            def _():
-                c_s[q, h] = r_s[q, h] * own + sp[hh]
-                c_ds[q, h] = r_ds[q, h] + oth * dsp[hh]
-
+        def join_lower(h, hh, own, oth):
+            c_s[q, h] = sp[hh] * oth + r_s[q, h]
+            c_ds[q, h] = dsp[hh] + own * r_ds[q, h]
+
+        def join_upper(h, hh, own, oth):
+            c_s[q, h] = r_s[q, h] * own + sp[hh]
+            c_ds[q, h] = r_ds[q, h] + oth * dsp[hh]
+
+        by_core(q, join_lower, join_upper)
         for c in chips:
             each(copies1(q, c, chip), "start")
         p_ld[q, chip] = c_ld[q]
 
-        @pl.loop(0, OWN)
-        def _(h):
+        for h in range(OWN):
             p_s[q, chip, h] = c_s[q, chip * OWN + h]
             p_ds[q, chip, h] = c_ds[q, chip * OWN + h]
 
@@ -211,8 +211,7 @@
             each(copies1(q, c, c), "wait_recv")
         t_ld[q] = sum(p_ld[q, c] for c in ALL_CHIPS)
 
-        @pl.loop(0, OWN)
-        def _(h):
+        for h in range(OWN):
             d = chip_decays(q, h)
             acc = p_s[q, 0, h]
             for c in ALL_CHIPS[1:]:
@@ -249,16 +248,17 @@
             copy2(q, 0, zz, zz).wait_recv()
         each(own_loads(q), "wait")
 
-        @pl.loop(0, OWN)
-        def _(h):
-            for zz in range(PLANES - 1):
-                @pl.when(zz < z)
-                def _():
+        for zz in range(PLANES - 1):
+            @pl.when(zz < z)
+            def _():
+                for h in range(OWN):
                     b_s[q, 0, h] = b_s[q, 0, h] * z_decay(q, zz, h) + z_b[q, zz, h]
-            for zz in range(PLANES)[:0:-1]:
-                @pl.when(zz > z)
-                def _():
+        for zz in range(PLANES)[:0:-1]:
+            @pl.when(zz > z)
+            def _():
+                for h in range(OWN):
                     b_ds[q, CHIPS - 1, h] = b_ds[q, CHIPS - 1, h] * z_decay(q, zz, h) + z_b[q, zz, h]
+        for h in range(OWN):
             d = chip_decays(q, h)
             acc = b_s[q, 0, h]
             for c in ALL_CHIPS[:-1]:
@@ -286,38 +286,34 @@
                 def _(h):
                     f_all[q, chip * OWN + h] = f_own[q, h]
 
-    def out_copies(q):
+    def out_copies(q, far_s, far_ds, near_s, near_ds):
         part = pl.ds(q * PIECE + mine, SHARE)
-        return [rcopy(o_s.at[q], start.at[part], send4.at[q, 0], recv4.at[q, 0], partner),
-                rcopy(o_ds.at[q], end.at[part], send4.at[q, 1], recv4.at[q, 1], partner),
-                pltpu.make_async_copy(n_s.at[q], start.at[part], loc.at[q, 2]),
-                pltpu.make_async_copy(n_ds.at[q], end.at[part], loc.at[q, 3])]
+        return [rcopy(far_s.at[q], start.at[part], send4.at[q, 0], recv4.at[q, 0], partner),
+                rcopy(far_ds.at[q], end.at[part], send4.at[q, 1], recv4.at[q, 1], partner),
+                pltpu.make_async_copy(near_s.at[q], start.at[part], loc.at[q, 2]),
+                pltpu.make_async_copy(near_ds.at[q], end.at[part], loc.at[q, 3])]
 
     def halve(q):
         for c in chips:
             each(copies3(q, c, c), "wait_recv")
 
-        @pl.loop(0, SHARE)
-        def _(h):
-            hh = q * PIECE + mine + h
-            own = jnp.exp2(ld[pl.ds(hh, 1), :])
-            oth = decay(r_ld, q, mine + h)
-
-            @pl.when(core == 0)
-            def _():
-                n_s[q, h] = a_s[q, h]
-                n_ds[q, h] = r_ds[q, h] + oth * a_ds[q, h]
-                o_s[q, h] = own * a_s[q, h] + sp[hh]
-                o_ds[q, h] = a_ds[q, h]
-
-            @pl.when(core == 1)
-            def _():
-                n_s[q, h] = oth * a_s[q, h] + r_s[q, h]
-                n_ds[q, h] = a_ds[q, h]
-                o_s[q, h] = a_s[q, h]
-                o_ds[q, h] = dsp[hh] + own * a_ds[q, h]
-
-        each(out_copies(q), "start")
+        def lower(h, hh, own, oth):
+            n_s[q, h] = own * a_s[q, h] + sp[hh]
+            n_ds[q, h] = r_ds[q, h] + oth * a_ds[q, h]
+
+        def upper(h, hh, own, oth):
+            n_s[q, h] = oth * a_s[q, h] + r_s[q, h]
+            n_ds[q, h] = dsp[hh] + own * a_ds[q, h]
+
+        by_core(q, lower, upper)
+
+        @pl.when(core == 0)
+        def _():
+            each(out_copies(q, n_s, a_ds, a_s, n_ds), "start")
+
+        @pl.when(core == 1)
+        def _():
+            each(out_copies(q, a_s, n_ds, n_s, a_ds), "start")
 
     def copy5(q, c_dst, c_slot):
         part = f_all.at[q, pl.ds(c_slot * OWN, OWN)]
@@ -345,7 +341,7 @@
                 copy5(q, c, c).wait_recv()
             each(last(q), "start")
         for q in range(QS):
-            each(out_copies(q), "wait")
+            each(out_copies(q, n_s, a_ds, a_s, n_ds), "wait")
             for c in chips:
                 each(copies1(q, c, chip) + copies3(q, c, chip) + [copy5(q, c, chip)], "wait_send")
             for zz in planes:
@@ -384,7 +380,7 @@
     three = D((QS, 3, CHIPS))
     two = D((QS, 2, CHIPS))
     return [share, share, logs(), share, share, logs(), four, four, logs(CHIPS), own, own, logs(), four, logs(PLANES),
-            four, four, share, share, share, share, share, share, own, share,
+            four, four, share, share, share, share, own, share,
             D((QS, 3)), D((QS, 3)), three, three, two, two, two, two, D((QS, 3)), D((QS, 3)), two, two, D((QS, 6))]
 
 
@@ -444,6 +440,17 @@
         dsp[g * GH + j] = acc_ds[blk(j, HD), :]
 
 
+def carry(state, weighted, k, other, tot, first):
+    upd = mm(weighted[k], cat0(other, other))
+    if first:
+        state[...] = upd
+        return
+    decay = jnp.exp2(tot)
+    for j in range(GH):
+        rows = blk(j, HD)
+        state[rows, :] = state[rows, :] * row(decay, j) + upd[rows, :]
+
+
 def local_group(nb, ng, g, late, x_ref, dy_ref, dt_ref, b_ref, c_ref, du_ref, ry_ref, db_ref, dc_ref,
                 gram, dgram, s_cur, ds_cur, xw, yw, y_in, u_in, rcol, cum_ref):
     @pl.when(g == 0)
@@ -456,9 +463,6 @@
         db_ref[...] = jnp.zeros_like(db_ref)
         dc_ref[...] = jnp.zeros_like(dc_ref)
         rcol[...] = jnp.zeros_like(rcol)
-
-    ds_cur[...] = jnp.zeros_like(ds_cur)
-    s_cur[...] = jnp.zeros_like(s_cur)
 
     @pl.loop(0, nb)
     def _(i):
@@ -476,47 +480,40 @@
             yw[i, rows, T:] = lo
             du_ref[rows, tok] = jnp.zeros((HD, T), F32)
 
-    @pl.loop(0, nb)
-    def _(i):
+    def block(i, first):
         for at_g, at_i, step in late:
-            @pl.when((g == at_g) & (i == at_i))
-            def _():
-                step()
+            if (at_i == 0) == first:
+                pl.when((g == at_g) if first else (g == at_g) & (i == at_i))(step)
 
         k = nb - 1 - i
-        tok_k = pl.ds(pl.multiple_of(k * T, T), T)
-        tok = pl.ds(pl.multiple_of(i * T, T), T)
+        tok_k, tok = (blk(k, T), blk(i, T)) if first else (pl.ds(pl.multiple_of(k * T, T), T), pl.ds(pl.multiple_of(i * T, T), T))
 
         cum_k = cum_ref[:, tok_k]
         tot_k = last_col(cum_k)
-        ds_hi, ds_lo = split2(ds_cur[...])
         b_k = b_ref[tok_k, :]
         c_k = c_ref[tok_k, :]
-        u_in[...] = mm_nt(cat1(ds_hi, ds_lo), cat1(b_k, b_k))
-        db2 = mm_tn(xw[k, :, :T], cat1(ds_hi, ds_lo))
-        db_ref[tok_k, :] += db2[:, :N] + db2[:, N:] + mm_tn(xw[k, :, T:], ds_hi)
-        upd_k = mm(yw[k], cat0(c_k, c_k))
-        e_in = jnp.exp2(tot_k - cum_k)
-        e_tot_k = jnp.exp2(tot_k)
-        for j in range(GH):
-            rows = blk(j, HD)
-            du_ref[rows, tok_k] += u_in[rows, :] * row(e_in, j)
-            ds_cur[rows, :] = ds_cur[rows, :] * row(e_tot_k, j) + upd_k[rows, :]
+        if not first:
+            ds_hi, ds_lo = split2(ds_cur[...])
+            u_in[...] = mm_nt(cat1(ds_hi, ds_lo), cat1(b_k, b_k))
+            db2 = mm_tn(xw[k, :, :T], cat1(ds_hi, ds_lo))
+            db_ref[tok_k, :] += db2[:, :N] + db2[:, N:] + mm_tn(xw[k, :, T:], ds_hi)
+            e_in = jnp.exp2(tot_k - cum_k)
+            for j in range(GH):
+                rows = blk(j, HD)
+                du_ref[rows, tok_k] += u_in[rows, :] * row(e_in, j)
+        carry(ds_cur, yw, k, c_k, tot_k, first)
 
         cum = cum_ref[:, tok]
-        e_tot = jnp.exp2(last_col(cum))
         e_out = jnp.exp2(cum)
         dt = dt_ref[:, tok]
-        s_hi, s_lo = split2(s_cur[...])
         b_i = b_ref[tok, :]
         c_i = c_ref[tok, :]
-        y_in[...] = mm_nt(cat1(s_hi, s_lo), cat1(c_i, c_i))
-        dc2 = mm_tn(yw[i, :, :T], cat1(s_hi, s_lo))
-        dc_ref[tok, :] += dc2[:, :N] + dc2[:, N:] + mm_tn(yw[i, :, T:], s_hi)
-        upd = mm(xw[i], cat0(b_i, b_i))
-        for j in range(GH):
-            rows = blk(j, HD)
-            s_cur[rows, :] = s_cur[rows, :] * row(e_tot, j) + upd[rows, :]
+        if not first:
+            s_hi, s_lo = split2(s_cur[...])
+            y_in[...] = mm_nt(cat1(s_hi, s_lo), cat1(c_i, c_i))
+            dc2 = mm_tn(yw[i, :, :T], cat1(s_hi, s_lo))
+            dc_ref[tok, :] += dc2[:, :N] + dc2[:, N:] + mm_tn(yw[i, :, T:], s_hi)
+        carry(s_cur, xw, i, b_i, last_col(cum), first)
         cum_c = jnp.transpose(cum)
         g_i = gram[i]
         zero = jnp.zeros((HD, T), BF16)
@@ -536,9 +533,17 @@
                 m_hi, m_lo = split2(m)
                 yb = dy_ref[rows, tok]
                 du_ref[rows, tok] += mm(cat1(yb, yb), cat0(m_hi, m_lo))
-                inter.append(sum0(yb.astype(F32) * y_in[rows, :]))
+                if not first:
+                    inter.append(sum0(yb.astype(F32) * y_in[rows, :]))
             dgram[i] += e_sum
-        ry_ref[:, tok] = jnp.transpose(rcol[...])[:GH, :] + e_out * cat0(*inter)
+        own = jnp.transpose(rcol[...])[:GH, :]
+        ry_ref[:, tok] = own + e_out * cat0(*inter) if inter else own
+
+    block(0, True)
+
+    @pl.loop(1, nb)
+    def _(i):
+        block(i, False)
 
     @pl.when(g == ng - 1)
     def _():

time: 133 us -> 128 us (0.962)
  Pallas kernels: 130 us -> 125 us
    pallas_call x1, Pallas kernels: 88.1 us -> 85.5 us  [local_grads(): pl.pallas_call(functools.partial(local_kernel, nb, ng), grid=(2 * ng,), i...]
    pallas_call x1, Pallas kernels: 16.9 us -> 15 us  [sum_devices(): pl.pallas_call(sum_kernel, in_specs=[vm, vm], out_specs=[vm, vm], out_sha...]
where the time goes in v4:
time: 128 us
  Pallas kernels  125 us (98%)
  local copies, waits for them, and re-layouts  2.32 us (2%)
    pallas_call x1, Pallas kernels, local_grads(): pl.pallas_call(functools.partial(local_kernel, nb, ng), grid=(2 * ng,), i...  85.5 us
    pallas_call x1, Pallas kernels, join_grads(): pl.pallas_call(functools.partial(join_kernel, nb, ng), grid=(ng,), in_spe...  24.6 us
    pallas_call x1, Pallas kernels, sum_devices(): pl.pallas_call(sum_kernel, in_specs=[vm, vm], out_specs=[vm, vm], out_sha...  15 us

profile of v4, /device:TPU:0, one launch (start us, length us, event | category | flops | bytes accessed | tf_op | source)
XLA Modules:
  0.0 128.1 jit_solution(8952314191894334252)
XLA Ops:
  0.6 85.5 %local_grads.1 = (f32[4096,768]{1,0:T(8,128)}, f32[64,768]{1,0:T(8,128)}, f32[768,128]{1,0:T(8,128)}, f32[768,128]{1,0:T(8,128)}, f32[64,768]{1,0:T(8,128)}, /*i...) custom-call(bf16[4096,768]{1,0:T(8,128)(2,1)} %bitcast.36, ...), custom_call_target="tpu_custom_call" | custom-call | tf_op jit(solution)/shard_map/local_grads/pallas_call | solution.py:575
  86.1 24.6 %join_grads.1 = (bf16[4096,768]{1,0:T(8,128)(2,1)}, f32[64,768]{1,0:T(8,128)}, f32[64,128]{1,0:T(8,128)}, f32[64,128]{1,0:T(8,128)}, bf16[768,128]{1,0:T(8,128)(...) custom-call(bf16[4096,768]{1,0:T(8,128)(2,1)} %bitcast.37, bf16[4096,768]{1,0:T(8,128)(2,1)} %bitcast.39, ...), custom_call_target="tpu_custom_call" | custom-call | tf_op jit(solution)/shard_map/join_grads/pallas_call | solution.py:689
  110.7 15.0 %sum_devices.1 = (f32[1,64]{1,0:T(1,128)}, f32[1,64]{1,0:T(1,128)}) custom-call(f32[64,128]{1,0:T(8,128)} %get-tuple-element.39.dal_ref, f32[64,128]{1,0:T(8,128)} %get-tuple-element.40.dsk_ref), custom_call_target="tpu_custom_call" | custom-call | tf_op jit(solution)/shard_map/sum_devices/pallas_call | solution.py:734
  125.8 1.2 copy.18
  127.0 1.1 copy.19

commit v5 on v4

--- a/solution.py
+++ b/solution.py
@@ -358,10 +358,7 @@
 
     early = {0: [hello], 4: [functools.partial(swap, 0)], 6: [functools.partial(pairs, 0)],
              8: [functools.partial(swap, 1), lambda: each(sp_copy(), "start")]}
-    late = [(0, 2, functools.partial(pairs, 1)), (1, 2, functools.partial(plane, 0)), (2, 5, functools.partial(plane, 1)),
-            (3, 0, functools.partial(prefix, 0)), (4, 3, functools.partial(prefix, 1)), (4, 3, send_first),
-            (5, 0, functools.partial(halve, 0)), (6, 2, functools.partial(halve, 1)), (6, 3, functools.partial(spread, 0)),
-            (6, 5, functools.partial(spread, 1)), (7, 5, finish)]
+    late = [(0, 1, functools.partial(pairs, 1)), (1, 3, functools.partial(plane, 0)), (3, 0, functools.partial(plane, 1)), (3, 3, functools.partial(prefix, 0)), (4, 5, functools.partial(prefix, 1)), (4, 5, send_first), (5, 2, functools.partial(halve, 0)), (6, 4, functools.partial(halve, 1)), (6, 4, functools.partial(spread, 0)), (7, 0, functools.partial(spread, 1)), (7, 5, finish)]
     return early, late
 
 
@@ -704,44 +701,55 @@
         name="join_grads",
     )(x_t, dy_t, dt_t, cum, a_log, d_skip, s0, dse, sp, b, c, du, ry, dbl, dcl, first)
 
-def sum_kernel(dal_ref, dsk_ref, al_ref, sk_ref, v1, v2, v3, send, recv):
-    core, chip, z, partner, chips, planes, at_chip, at_z = neighbours()
-    greet(partner, chips, planes, at_chip, at_z)
-    v1[core] = cat0(jnp.transpose(dal_ref[...])[:OWN, :], jnp.transpose(dsk_ref[...])[:OWN, :])
-    met(chips, planes)
-
-    def copy(buf, stage, to, slot, dev):
-        return rcopy(buf.at[slot], buf.at[slot], send.at[stage, to], recv.at[stage, slot], dev)
-
-    def exchange(buf, stage, me, others, at):
-        each([copy(buf, stage, o, me, at(o)) for o in others], "start")
-        each([copy(buf, stage, o, o, at(o)) for o in others], "wait_recv")
-        each([copy(buf, stage, o, me, at(o)) for o in others], "wait_send")
-
-    exchange(v1, 0, core, [1 - core], lambda o: partner)
-    v2[chip] = v1[0] + v1[1]
-    exchange(v2, 1, chip, chips, at_chip)
-    v3[z] = sum(v2[c] for c in ALL_CHIPS)
-    exchange(v3, 2, z, planes, at_z)
-    total = sum(v3[p] for p in range(PLANES))
-    al_ref[...] = row(total, 0)
-    sk_ref[...] = row(total, OWN)
+HALF_ROWS = GH // 2
+IN_PLANE = 2 * CHIPS
+
+
+def sum_kernel(dal_ref, dsk_ref, out_ref, v1, v2, send, recv):
+    me = lax.axis_index(AXIS)
+    pos, z = lax.rem(me, IN_PLANE), me // IN_PLANE
+    near = [lax.rem(pos + r, IN_PLANE) for r in range(1, IN_PLANE)]
+    far = [lax.rem(z + r, PLANES) for r in range(1, PLANES)]
+
+    def at_pos(o):
+        return me + o - pos
+
+    def at_z(o):
+        return me + IN_PLANE * (o - z)
+
+    barrier = pltpu.get_barrier_semaphore()
+    for p in [at_pos(o) for o in near] + [at_z(o) for o in far]:
+        pl.semaphore_signal(barrier, inc=1, device_id=(p,), device_id_type=MESH)
+    v1[pos] = cat0(jnp.transpose(dal_ref[...])[:HALF_ROWS, :], jnp.transpose(dsk_ref[...])[:HALF_ROWS, :])
+    pl.semaphore_wait(barrier, len(near) + len(far))
+
+    def exchange(buf, stage, own, others, at):
+        def copy(to, slot, dev):
+            return rcopy(buf.at[slot], buf.at[slot], send.at[stage, to], recv.at[stage, slot], dev)
+
+        each([copy(o, own, at(o)) for o in others], "start")
+        each([copy(o, o, at(o)) for o in others], "wait_recv")
+        each([copy(o, own, at(o)) for o in others], "wait_send")
+
+    exchange(v1, 0, pos, near, at_pos)
+    v2[z] = sum(v1[o] for o in range(IN_PLANE))
+    exchange(v2, 1, z, far, at_z)
+    out_ref[...] = sum(v2[o] for o in range(PLANES))
 
 
 def sum_devices(dal, dsk):
     vm = pl.BlockSpec(memory_space=pltpu.VMEM)
-    V = pltpu.VMEM
-    al, sk = pl.pallas_call(
+    out = pl.pallas_call(
         sum_kernel,
         in_specs=[vm, vm],
-        out_specs=[vm, vm],
-        out_shape=[jax.ShapeDtypeStruct((1, HEADS), F32)] * 2,
-        scratch_shapes=[V((2, 2 * OWN, HEADS), F32), V((CHIPS, 2 * OWN, HEADS), F32), V((PLANES, 2 * OWN, HEADS), F32),
-                        pltpu.SemaphoreType.DMA((3, CHIPS)), pltpu.SemaphoreType.DMA((3, CHIPS))],
+        out_specs=vm,
+        out_shape=jax.ShapeDtypeStruct((GH, HEADS), F32),
+        scratch_shapes=[pltpu.VMEM((IN_PLANE, GH, HEADS), F32), pltpu.VMEM((PLANES, GH, HEADS), F32),
+                        pltpu.SemaphoreType.DMA((2, IN_PLANE)), pltpu.SemaphoreType.DMA((2, IN_PLANE))],
         compiler_params=pltpu.CompilerParams(collective_id=1, has_side_effects=True),
         name="sum_devices",
     )(dal, dsk)
-    return al[0], sk[0]
+    return out[0], out[HALF_ROWS]
 
 
 def solution(mesh):

time: 128 us -> 126 us (0.984)
    unnamed x2 -> x0, local copies, waits for them, and re-layouts: 2.32 us -> none
    pallas_call x1, Pallas kernels: 15 us -> 13.4 us  [sum_devices(): pl.pallas_call(sum_kernel, in_specs=[vm, vm], out_specs=vm, out_shape=jax...]
where the time goes in v5:
time: 126 us
  Pallas kernels  124 us (98%)
  local copies, waits for them, and re-layouts  1.27 us (1%)
    pallas_call x1, Pallas kernels, local_grads(): pl.pallas_call(functools.partial(local_kernel, nb, ng), grid=(2 * ng,), i...  85.8 us
    pallas_call x1, Pallas kernels, join_grads(): pl.pallas_call(functools.partial(join_kernel, nb, ng), grid=(ng,), in_spe...  24.6 us
    pallas_call x1, Pallas kernels, sum_devices(): pl.pallas_call(sum_kernel, in_specs=[vm, vm], out_specs=vm, out_shape=jax...  13.4 us

profile of v5, /device:TPU:0, one launch (start us, length us, event | category | flops | bytes accessed | tf_op | source)
XLA Modules:
  0.0 125.8 jit_solution(10950925186662617478)
XLA Ops:
  0.6 85.8 %local_grads.1 = (f32[4096,768]{1,0:T(8,128)}, f32[64,768]{1,0:T(8,128)}, f32[768,128]{1,0:T(8,128)}, f32[768,128]{1,0:T(8,128)}, f32[64,768]{1,0:T(8,128)}, /*i...) custom-call(bf16[4096,768]{1,0:T(8,128)(2,1)} %bitcast.38, ...), custom_call_target="tpu_custom_call" | custom-call | tf_op jit(solution)/shard_map/local_grads/pallas_call | solution.py:572
  86.5 24.6 %join_grads.1 = (bf16[4096,768]{1,0:T(8,128)(2,1)}, f32[64,768]{1,0:T(8,128)}, f32[64,128]{1,0:T(8,128)}, f32[64,128]{1,0:T(8,128)}, bf16[768,128]{1,0:T(8,128)(...) custom-call(bf16[4096,768]{1,0:T(8,128)(2,1)} %bitcast.39, bf16[4096,768]{1,0:T(8,128)(2,1)} %bitcast.41, ...), custom_call_target="tpu_custom_call" | custom-call | tf_op jit(solution)/shard_map/join_grads/pallas_call | solution.py:686
  111.1 13.4 %sum_devices.1 = f32[8,64]{1,0:T(8,128)} custom-call(f32[64,128]{1,0:T(8,128)} %get-tuple-element.37.dal_ref, f32[64,128]{1,0:T(8,128)} %get-tuple-element.38.dsk_ref), custom_call_target="tpu_custom_call" | custom-call | tf_op jit(solution)/shard_map/sum_devices/pallas_call | solution.py:742
  124.5 1.3 %slice_bitcast_fusion = (f32[64]{0:T(128)}, f32[64]{0:T(128)}) fusion(f32[8,64]{1,0:T(8,128)} %sum_devices.1), kind=kLoop, calls=%fused_computation | loop fusion | bytes 1024 | tf_op jit(solution)/shard_map/squeeze | solution.py:752
